TPU v7x, 256 devices: a whole 4x4x8 slice. The times are simulated.
256 devices in a mesh: rep: 32 (over z_hi, y, x), dom: 8 (over z_lo, core).
Axes of the slice: x: 4, y: 4, z: 8 (z_hi: 2, z_lo: 4; z = z_hi * 4 + z_lo), core: 2. Of those that a mesh axis runs over, the one named last changes fastest.
Arguments:
- protein_pos: float32 [3, 524288], P(None, ('rep', 'dom')), parts along dimension 1, may hold values from -4 to 4, as said below
- protein_vel: float32 [3, 524288], P(None, ('rep', 'dom')), parts along dimension 1, may hold values from -3 to 3
- inv_mass: float32 [524288], P(('rep', 'dom')), parts along dimension 0, may hold values from 0.0625 to 1
- bond_atoms: int32 [2, 327680], P(None, ('rep', 'dom')), parts along dimension 1, may hold values from 0 to 2047, as said below
- left_atoms: int32 [98304], P(('rep', 'dom')), parts along dimension 0, may hold values from 0 to 2047, as said below
- right_atoms: int32 [98304], P(('rep', 'dom')), parts along dimension 0, may hold values from 0 to 2047, as said below
- water_pos: float32 [9, 262144], P(None, ('rep', 'dom')), parts along dimension 1, may hold values from -3.2 to 3.2, as said below
- water_vel: float32 [9, 262144], P(None, ('rep', 'dom')), parts along dimension 1, may hold values from -3 to 3
Outputs:
- protein_velocity: float32 [3, 524288], P(None, ('rep', 'dom')), parts along dimension 1
- water_velocity: float32 [9, 262144], P(None, ('rep', 'dom')), parts along dimension 1
There are 32 independent parts, one for each index of `rep`. A program takes and returns all parts, laid end to end along the dimension named above; each array names one. Nothing has to cross between parts.
Inputs may be any that keep to these rules, and one draw needn't show every extreme that they name: `bond_atoms`: indices within the domain's block of 2048 atoms; each column joins two different atoms; together with the cross bonds the bonds form a forest. `left_atoms`: distinct indices within the domain's block, none of them in right_atoms. `right_atoms`: distinct indices within the domain's block. `protein_pos`: every bond and every cross bond joins atoms 0.1 to 0.15 apart. `water_pos`: each column holds one rigid water: oxygen, then two hydrogens, 0.09572 from the oxygen and 0.15139 from each other.
All inputs are finite; a program needn't handle non-finite values.
Results may differ from a plain program's by a relative error of at most 0.0003.
Values sent between devices are 32-bit elements; how exact they have to be, the bound alone decides.
No kernel may reach another device: no remote copies, remote signals or barrier semaphores. Data moves between devices by JAX's collectives and lax.ppermute only.
A program may use at most 64 MiB of HBM per device.

v0:
```python
import math

import jax
import jax.numpy as jnp
from jax import lax
from jax.sharding import PartitionSpec as P

ORDER = 4
ITER = 2


time_step = 0.002
mass_oxygen = 15.9994
mass_hydrogen = 1.008
oxygen_hydrogen = 0.09572
hydrogen_pair = 0.15139
total_mass = mass_oxygen + 2.0 * mass_hydrogen
half_pair = 0.5 * hydrogen_pair
water_height = math.sqrt(oxygen_hydrogen * oxygen_hydrogen - half_pair * half_pair)
oxygen_reach = 2.0 * mass_hydrogen * water_height / total_mass
hydrogen_reach = water_height - oxygen_reach


def shifted(value, axis, steps):
    count = lax.axis_size(axis)
    pairs = [(source, (source + steps) % count) for source in range(count)]
    return lax.ppermute(value, axis, pairs)


def cross_product(left, right):
    return jnp.stack(
        [
            left[1] * right[2] - left[2] * right[1],
            left[2] * right[0] - left[0] * right[2],
            left[0] * right[1] - left[1] * right[0],
        ]
    )


def inner(left, right):
    return jnp.sum(left * right, axis=0)


def settle(before, after):
    old_oxygen, old_first, old_second = (before[0:3], before[3:6], before[6:9])
    new_oxygen, new_first, new_second = (after[0:3], after[3:6], after[6:9])
    center = (mass_oxygen * new_oxygen + mass_hydrogen * (new_first + new_second)) / total_mass
    old_b = old_first - old_oxygen
    old_c = old_second - old_oxygen
    rel_a = new_oxygen - center
    rel_b = new_first - center
    rel_c = new_second - center
    normal = cross_product(old_b, old_c)
    side = cross_product(rel_a, normal)
    upward = cross_product(normal, side)
    axis_z = normal / jnp.sqrt(inner(normal, normal))
    axis_x = side / jnp.sqrt(inner(side, side))
    axis_y = upward / jnp.sqrt(inner(upward, upward))
    oldb_x = inner(axis_x, old_b)
    oldb_y = inner(axis_y, old_b)
    oldc_x = inner(axis_x, old_c)
    oldc_y = inner(axis_y, old_c)
    newa_z = inner(axis_z, rel_a)
    newb_x = inner(axis_x, rel_b)
    newb_y = inner(axis_y, rel_b)
    newb_z = inner(axis_z, rel_b)
    newc_x = inner(axis_x, rel_c)
    newc_y = inner(axis_y, rel_c)
    newc_z = inner(axis_z, rel_c)
    sin_phi = newa_z / oxygen_reach
    cos_phi = jnp.sqrt(1.0 - sin_phi * sin_phi)
    sin_psi = (newb_z - newc_z) / (2.0 * half_pair * cos_phi)
    cos_psi = jnp.sqrt(1.0 - sin_psi * sin_psi)
    rest_ay = oxygen_reach * cos_phi
    rest_bx = -half_pair * cos_psi
    lowered = -hydrogen_reach * cos_phi
    tilted = half_pair * sin_psi * sin_phi
    rest_by = lowered - tilted
    rest_cy = lowered + tilted
    alpha = rest_bx * (oldb_x - oldc_x) + oldb_y * rest_by + oldc_y * rest_cy
    beta = rest_bx * (oldc_y - oldb_y) + oldb_x * rest_by + oldc_x * rest_cy
    gamma = oldb_x * newb_y - newb_x * oldb_y + oldc_x * newc_y - newc_x * oldc_y
    summed = alpha * alpha + beta * beta
    sin_theta = (alpha * gamma - beta * jnp.sqrt(summed - gamma * gamma)) / summed
    cos_theta = jnp.sqrt(1.0 - sin_theta * sin_theta)
    final_ax = -rest_ay * sin_theta
    final_ay = rest_ay * cos_theta
    final_bx = rest_bx * cos_theta - rest_by * sin_theta
    final_by = rest_bx * sin_theta + rest_by * cos_theta
    final_cx = -rest_bx * cos_theta - rest_cy * sin_theta
    final_cy = -rest_bx * sin_theta + rest_cy * cos_theta
    oxygen = center + axis_x * final_ax + axis_y * final_ay + axis_z * newa_z
    first = center + axis_x * final_bx + axis_y * final_by + axis_z * newb_z
    second = center + axis_x * final_cx + axis_y * final_cy + axis_z * newc_z
    return jnp.concatenate([oxygen, first, second], axis=0)


def solve_bonds(old_ext, moved_ext, mass_ext, first, second, count, atom_field):
    diff = old_ext[:, first] - old_ext[:, second]
    length = jnp.sqrt(inner(diff, diff))
    unit = diff / length
    scale = 1.0 / jnp.sqrt(mass_ext[first] + mass_ext[second])
    delta = jnp.zeros_like(moved_ext)
    rhs = scale * (inner(unit, moved_ext[:, first] - moved_ext[:, second]) - length)
    for round_index in range(ITER + 1):
        if round_index > 0:
            now = moved_ext + delta
            gap = now[:, first] - now[:, second]
            target = jnp.sqrt(2.0 * length * length - inner(gap, gap))
            rhs = scale * (length - target)
        total = rhs
        current = rhs
        for order_index in range(ORDER):
            field = atom_field(unit * (scale * current), True)
            current = current - scale * inner(unit, field[:, first] - field[:, second])
            total = total + current
        if round_index == ITER:
            return delta[:, :count] - atom_field(unit * (scale * total), False)
        delta = delta - atom_field(unit * (scale * total), True)


def on_device(
    protein_pos, protein_vel, inv_mass, bond_atoms, left_atoms, right_atoms, water_pos, water_vel
):
    count = protein_pos.shape[1]
    halo = left_atoms.shape[0]
    moved = protein_pos + time_step * protein_vel
    slots = jnp.arange(halo, dtype=jnp.int32)
    cap_data = jnp.concatenate(
        [protein_pos[:, left_atoms], moved[:, left_atoms], inv_mass[left_atoms][None]], axis=0
    )
    caps = shifted(cap_data, "dom", -1)
    old_ext = jnp.concatenate([protein_pos, caps[0:3]], axis=1)
    moved_ext = jnp.concatenate([moved, caps[3:6]], axis=1)
    mass_ext = jnp.concatenate([inv_mass, caps[6]])
    first = jnp.concatenate([bond_atoms[0], right_atoms])
    second = jnp.concatenate([bond_atoms[1], count + slots])

    def atom_field(weighted, edges):
        force = (
            jnp.zeros((3, count + halo), jnp.float32)
            .at[:, first]
            .add(weighted)
            .at[:, second]
            .add(-weighted)
        )
        returned = shifted(force[:, count:], "dom", 1)
        own_field = inv_mass * force[:, :count].at[:, left_atoms].add(returned)
        if edges:
            edge_field = shifted(own_field[:, left_atoms], "dom", -1)
            return jnp.concatenate([own_field, edge_field], axis=1)
        return own_field

    water_moved = water_pos + time_step * water_vel
    settled = settle(water_pos, water_moved)
    water_velocity = water_vel + (settled - water_moved) / time_step
    delta = solve_bonds(old_ext, moved_ext, mass_ext, first, second, count, atom_field)
    protein_velocity = protein_vel + delta / time_step
    return (protein_velocity, water_velocity)


def solution(mesh):
    in_specs = (
        P(None, ("rep", "dom")),
        P(None, ("rep", "dom")),
        P(("rep", "dom")),
        P(None, ("rep", "dom")),
        P(("rep", "dom")),
        P(("rep", "dom")),
        P(None, ("rep", "dom")),
        P(None, ("rep", "dom")),
    )
    out_specs = (P(None, ("rep", "dom")), P(None, ("rep", "dom")))
    return jax.shard_map(
        on_device, mesh=mesh, in_specs=in_specs, out_specs=out_specs, check_vma=False
    )
```

profile of v0, /device:TPU:1, one launch (start us, length us, event | category | flops | bytes accessed | tf_op | source)
XLA Modules:
  0.0 788.1 jit_solution(10719165229786931957)
XLA Ops:
  11.7 9.1 %gather_fusion.6 = f32[1664]{0:T(1024)S(1)} fusion(f32[2432]{0:T(1024)S(1)} %pad_maximum_fusion.18, s32[2048]{0:T(1024)S(1)} %pad_clamp_fusion), kind=kCustom, calls=%fused_computation.6 | custom fusion | bytes 19968 | tf_op jit(solution)/shard_map/gather | solution.py:102
  20.8 9.1 %gather_fusion.5 = f32[1664]{0:T(1024)S(1)} fusion(f32[2432]{0:T(1024)S(1)} %pad_maximum_fusion.18, s32[2048]{0:T(1024)S(1)} %pad_clamp_fusion.1), kind=kCustom, calls=%fused_computation.5 | custom fusion | bytes 19968 | tf_op jit(solution)/shard_map/gather | solution.py:102
  49.7 13.0 %scatter_custom_fusion = f32[3,2432]{0,1:T(8,128)S(1)} fusion(s32[1664]{0:T(1024)S(1)} %get-tuple-element.68, f32[]{:T(128)} %constant.17.clone.1, f32[1664]{0:T(1024)S(1)} %get-tuple-element.49, f32[1664,3]{1,0:T(8,128)S(1)} %get-tuple-element.53, f32[1664]{0:T(1024)S(1)} %sqrt.199), kind=kCustom, calls=%fused_computation.185 | custom fusion | flops 14976 | bytes 897540 | tf_op jit(solution)/shard_map/scatter-add | solution.py:143
  62.6 13.3 %scatter_custom_fusion.1 = f32[3,2432]{0,1:T(8,128)S(1)} fusion(f32[3,2432]{0,1:T(8,128)S(1)} %scatter_custom_fusion, s32[1664]{0:T(1024)S(1)} %get-tuple-element.69, f32[1664]{0:T(1024)S(1)} %get-tuple-element.49, f32[1664,3]{1,0:T(8,128)S(1)} %get-tuple-element.53, f32[1664]{0:T(1024)S(1)} %sqrt.199), kind=kCustom, calls=%fused_computation.125 | custom fusion | flops 19968 | bytes 897536 | tf_op jit(solution)/shard_map/scatter-add | solution.py:145
  101.6 13.0 %scatter_custom_fusion.3 = f32[3,2432]{0,1:T(8,128)S(1)} fusion(s32[1664]{0:T(1024)S(1)} %get-tuple-element.68, f32[]{:T(128)} %constant.17.clone.1, f32[1664]{0:T(1024)S(1)} %fusion.163, f32[1664,3]{1,0:T(8,128)S(1)} %get-tuple-element.53, f32[1664]{0:T(1024)S(1)} %sqrt.199), kind=kCustom, calls=%fused_computation.182 | custom fusion | flops 14976 | bytes 897540 | tf_op jit(solution)/shard_map/scatter-add | solution.py:143
  114.6 13.3 %scatter_custom_fusion.4 = f32[3,2432]{0,1:T(8,128)S(1)} fusion(f32[3,2432]{0,1:T(8,128)S(1)} %scatter_custom_fusion.3, s32[1664]{0:T(1024)S(1)} %get-tuple-element.69, f32[1664]{0:T(1024)S(1)} %fusion.163, f32[1664,3]{1,0:T(8,128)S(1)} %get-tuple-element.53, f32[1664]{0:T(1024)S(1)} %sqrt.199), kind=kCustom, calls=%fused_computation.123 | custom fusion | flops 19968 | bytes 897536 | tf_op jit(solution)/shard_map/scatter-add | solution.py:145
  151.8 13.0 %scatter_custom_fusion.6 = f32[3,2432]{0,1:T(8,128)S(1)} fusion(s32[1664]{0:T(1024)S(1)} %get-tuple-element.68, f32[]{:T(128)} %constant.17.clone.1, f32[1664]{0:T(1024)S(1)} %fusion.167, f32[1664,3]{1,0:T(8,128)S(1)} %get-tuple-element.53, f32[1664]{0:T(1024)S(1)} %sqrt.199), kind=kCustom, calls=%fused_computation.179 | custom fusion | flops 14976 | bytes 897540 | tf_op jit(solution)/shard_map/scatter-add | solution.py:143
  164.7 13.3 %scatter_custom_fusion.7 = f32[3,2432]{0,1:T(8,128)S(1)} fusion(f32[3,2432]{0,1:T(8,128)S(1)} %scatter_custom_fusion.6, s32[1664]{0:T(1024)S(1)} %get-tuple-element.69, f32[1664]{0:T(1024)S(1)} %fusion.167, f32[1664,3]{1,0:T(8,128)S(1)} %get-tuple-element.53, f32[1664]{0:T(1024)S(1)} %sqrt.199), kind=kCustom, calls=%fused_computation.121 | custom fusion | flops 19968 | bytes 897536 | tf_op jit(solution)/shard_map/scatter-add | solution.py:145
  201.6 13.0 %scatter_custom_fusion.9 = f32[3,2432]{0,1:T(8,128)S(1)} fusion(s32[1664]{0:T(1024)S(1)} %get-tuple-element.68, f32[]{:T(128)} %constant.17.clone.1, f32[1664]{0:T(1024)S(1)} %fusion.158, f32[1664,3]{1,0:T(8,128)S(1)} %get-tuple-element.53, f32[1664]{0:T(1024)S(1)} %sqrt.199), kind=kCustom, calls=%fused_computation.176 | custom fusion | flops 14976 | bytes 897540 | tf_op jit(solution)/shard_map/scatter-add | solution.py:143
  214.6 13.3 %scatter_custom_fusion.10 = f32[3,2432]{0,1:T(8,128)S(1)} fusion(f32[3,2432]{0,1:T(8,128)S(1)} %scatter_custom_fusion.9, s32[1664]{0:T(1024)S(1)} %get-tuple-element.69, f32[1664]{0:T(1024)S(1)} %fusion.158, f32[1664,3]{1,0:T(8,128)S(1)} %get-tuple-element.53, f32[1664]{0:T(1024)S(1)} %sqrt.199), kind=kCustom, calls=%fused_computation.119 | custom fusion | flops 19968 | bytes 897536 | tf_op jit(solution)/shard_map/scatter-add | solution.py:145
  251.6 13.0 %scatter_custom_fusion.12 = f32[3,2432]{0,1:T(8,128)S(1)} fusion(s32[1664]{0:T(1024)S(1)} %get-tuple-element.68, f32[]{:T(128)} %constant.17.clone.1, f32[1664]{0:T(1024)S(1)} %add_multiply_fusion.3, f32[1664,3]{1,0:T(8,128)S(1)} %get-tuple-element.53, f32[1664]{0:T(1024)S(1)} %sqrt.199), kind=kCustom, calls=%fused_computation.173 | custom fusion | flops 14976 | bytes 897540 | tf_op jit(solution)/shard_map/scatter-add | solution.py:143
  264.6 13.3 %scatter_custom_fusion.13 = f32[3,2432]{0,1:T(8,128)S(1)} fusion(f32[3,2432]{0,1:T(8,128)S(1)} %scatter_custom_fusion.12, s32[1664]{0:T(1024)S(1)} %get-tuple-element.69, f32[1664]{0:T(1024)S(1)} %add_multiply_fusion.3, f32[1664,3]{1,0:T(8,128)S(1)} %get-tuple-element.53, f32[1664]{0:T(1024)S(1)} %sqrt.199), kind=kCustom, calls=%fused_computation.117 | custom fusion | flops 19968 | bytes 897536 | tf_op jit(solution)/shard_map/scatter-add | solution.py:145
  301.8 13.0 %scatter_custom_fusion.15 = f32[3,2432]{0,1:T(8,128)S(1)} fusion(s32[1664]{0:T(1024)S(1)} %get-tuple-element.68, f32[]{:T(128)} %constant.17.clone.1, f32[1664]{0:T(1024)S(1)} %get-tuple-element.47, f32[1664,3]{1,0:T(8,128)S(1)} %get-tuple-element.53, f32[1664]{0:T(1024)S(1)} %sqrt.199), kind=kCustom, calls=%fused_computation.170 | custom fusion | flops 14976 | bytes 897540 | tf_op jit(solution)/shard_map/scatter-add | solution.py:143
  314.8 13.3 %scatter_custom_fusion.16 = f32[3,2432]{0,1:T(8,128)S(1)} fusion(f32[3,2432]{0,1:T(8,128)S(1)} %scatter_custom_fusion.15, s32[1664]{0:T(1024)S(1)} %get-tuple-element.69, f32[1664]{0:T(1024)S(1)} %get-tuple-element.47, f32[1664,3]{1,0:T(8,128)S(1)} %get-tuple-element.53, f32[1664]{0:T(1024)S(1)} %sqrt.199), kind=kCustom, calls=%fused_computation.115 | custom fusion | flops 19968 | bytes 897536 | tf_op jit(solution)/shard_map/scatter-add | solution.py:145
  353.4 13.0 %scatter_custom_fusion.18 = f32[3,2432]{0,1:T(8,128)S(1)} fusion(s32[1664]{0:T(1024)S(1)} %get-tuple-element.68, f32[]{:T(128)} %constant.17.clone.1, f32[1664]{0:T(1024)S(1)} %fusion.164, f32[1664,3]{1,0:T(8,128)S(1)} %get-tuple-element.53, f32[1664]{0:T(1024)S(1)} %sqrt.199), kind=kCustom, calls=%fused_computation.167 | custom fusion | flops 14976 | bytes 897540 | tf_op jit(solution)/shard_map/scatter-add | solution.py:143
  366.4 13.3 %scatter_custom_fusion.19 = f32[3,2432]{0,1:T(8,128)S(1)} fusion(f32[3,2432]{0,1:T(8,128)S(1)} %scatter_custom_fusion.18, s32[1664]{0:T(1024)S(1)} %get-tuple-element.69, f32[1664]{0:T(1024)S(1)} %fusion.164, f32[1664,3]{1,0:T(8,128)S(1)} %get-tuple-element.53, f32[1664]{0:T(1024)S(1)} %sqrt.199), kind=kCustom, calls=%fused_computation.113 | custom fusion | flops 19968 | bytes 897536 | tf_op jit(solution)/shard_map/scatter-add | solution.py:145
  403.4 13.0 %scatter_custom_fusion.21 = f32[3,2432]{0,1:T(8,128)S(1)} fusion(s32[1664]{0:T(1024)S(1)} %get-tuple-element.68, f32[]{:T(128)} %constant.17.clone.1, f32[1664]{0:T(1024)S(1)} %fusion.168, f32[1664,3]{1,0:T(8,128)S(1)} %get-tuple-element.53, f32[1664]{0:T(1024)S(1)} %sqrt.199), kind=kCustom, calls=%fused_computation.164 | custom fusion | flops 14976 | bytes 897540 | tf_op jit(solution)/shard_map/scatter-add | solution.py:143
  416.3 13.3 %scatter_custom_fusion.22 = f32[3,2432]{0,1:T(8,128)S(1)} fusion(f32[3,2432]{0,1:T(8,128)S(1)} %scatter_custom_fusion.21, s32[1664]{0:T(1024)S(1)} %get-tuple-element.69, f32[1664]{0:T(1024)S(1)} %fusion.168, f32[1664,3]{1,0:T(8,128)S(1)} %get-tuple-element.53, f32[1664]{0:T(1024)S(1)} %sqrt.199), kind=kCustom, calls=%fused_computation.111 | custom fusion | flops 19968 | bytes 897536 | tf_op jit(solution)/shard_map/scatter-add | solution.py:145
  453.5 13.0 %scatter_custom_fusion.24 = f32[3,2432]{0,1:T(8,128)S(1)} fusion(s32[1664]{0:T(1024)S(1)} %get-tuple-element.68, f32[]{:T(128)} %constant.17.clone.1, f32[1664]{0:T(1024)S(1)} %fusion.159, f32[1664,3]{1,0:T(8,128)S(1)} %get-tuple-element.53, f32[1664]{0:T(1024)S(1)} %sqrt.199), kind=kCustom, calls=%fused_computation.161 | custom fusion | flops 14976 | bytes 897540 | tf_op jit(solution)/shard_map/scatter-add | solution.py:143
  466.5 13.3 %scatter_custom_fusion.25 = f32[3,2432]{0,1:T(8,128)S(1)} fusion(f32[3,2432]{0,1:T(8,128)S(1)} %scatter_custom_fusion.24, s32[1664]{0:T(1024)S(1)} %get-tuple-element.69, f32[1664]{0:T(1024)S(1)} %fusion.159, f32[1664,3]{1,0:T(8,128)S(1)} %get-tuple-element.53, f32[1664]{0:T(1024)S(1)} %sqrt.199), kind=kCustom, calls=%fused_computation.109 | custom fusion | flops 19968 | bytes 897536 | tf_op jit(solution)/shard_map/scatter-add | solution.py:145
  503.4 13.0 %scatter_custom_fusion.27 = f32[3,2432]{0,1:T(8,128)S(1)} fusion(s32[1664]{0:T(1024)S(1)} %get-tuple-element.68, f32[]{:T(128)} %constant.17.clone.1, f32[1664]{0:T(1024)S(1)} %add_multiply_fusion.2, f32[1664,3]{1,0:T(8,128)S(1)} %get-tuple-element.53, f32[1664]{0:T(1024)S(1)} %sqrt.199), kind=kCustom, calls=%fused_computation.158 | custom fusion | flops 14976 | bytes 897540 | tf_op jit(solution)/shard_map/scatter-add | solution.py:143
  516.4 13.3 %scatter_custom_fusion.28 = f32[3,2432]{0,1:T(8,128)S(1)} fusion(f32[3,2432]{0,1:T(8,128)S(1)} %scatter_custom_fusion.27, s32[1664]{0:T(1024)S(1)} %get-tuple-element.69, f32[1664]{0:T(1024)S(1)} %add_multiply_fusion.2, f32[1664,3]{1,0:T(8,128)S(1)} %get-tuple-element.53, f32[1664]{0:T(1024)S(1)} %sqrt.199), kind=kCustom, calls=%fused_computation.107 | custom fusion | flops 19968 | bytes 897536 | tf_op jit(solution)/shard_map/scatter-add | solution.py:145
  553.1 13.1 %scatter_custom_fusion.30 = f32[3,2432]{0,1:T(8,128)S(1)} fusion(s32[1664]{0:T(1024)} %copy-done.31, f32[]{:T(128)} %constant.17.clone.1, f32[1664]{0:T(1024)S(1)} %get-tuple-element.43, f32[1664,3]{1,0:T(8,128)S(1)} %get-tuple-element.53, f32[1664]{0:T(1024)S(1)} %sqrt.199), kind=kCustom, calls=%fused_computation.155 | custom fusion | flops 14976 | bytes 62976 | tf_op jit(solution)/shard_map/scatter-add | solution.py:143
  566.3 13.4 %scatter_custom_fusion.31 = f32[3,2432]{0,1:T(8,128)S(1)} fusion(f32[3,2432]{0,1:T(8,128)S(1)} %scatter_custom_fusion.30, s32[1664]{0:T(1024)} %copy-done.30, f32[1664]{0:T(1024)S(1)} %get-tuple-element.43, f32[1664,3]{1,0:T(8,128)S(1)} %get-tuple-element.53, f32[1664]{0:T(1024)S(1)} %sqrt.199), kind=kCustom, calls=%fused_computation.105 | custom fusion | flops 19968 | bytes 897536 | tf_op jit(solution)/shard_map/scatter-add | solution.py:145
  603.5 13.1 %scatter_custom_fusion.33 = f32[3,2432]{0,1:T(8,128)S(1)} fusion(s32[1664]{0:T(1024)} %copy-done.31, f32[]{:T(128)} %constant.17.clone.1, f32[1664]{0:T(1024)S(1)} %fusion.165, f32[1664,3]{1,0:T(8,128)S(1)} %get-tuple-element.53, f32[1664]{0:T(1024)S(1)} %sqrt.199), kind=kCustom, calls=%fused_computation.152 | custom fusion | flops 14976 | bytes 62976 | tf_op jit(solution)/shard_map/scatter-add | solution.py:143
  616.6 13.4 %scatter_custom_fusion.34 = f32[3,2432]{0,1:T(8,128)S(1)} fusion(f32[3,2432]{0,1:T(8,128)S(1)} %scatter_custom_fusion.33, s32[1664]{0:T(1024)} %copy-done.30, f32[1664]{0:T(1024)S(1)} %fusion.165, f32[1664,3]{1,0:T(8,128)S(1)} %get-tuple-element.53, f32[1664]{0:T(1024)S(1)} %sqrt.199), kind=kCustom, calls=%fused_computation.103 | custom fusion | flops 19968 | bytes 897536 | tf_op jit(solution)/shard_map/scatter-add | solution.py:145
  653.7 13.1 %scatter_custom_fusion.36 = f32[3,2432]{0,1:T(8,128)S(1)} fusion(s32[1664]{0:T(1024)} %copy-done.31, f32[]{:T(128)} %constant.17.clone.1, f32[1664]{0:T(1024)S(1)} %fusion.169, f32[1664,3]{1,0:T(8,128)S(1)} %get-tuple-element.53, f32[1664]{0:T(1024)S(1)} %sqrt.199), kind=kCustom, calls=%fused_computation.149 | custom fusion | flops 14976 | bytes 62976 | tf_op jit(solution)/shard_map/scatter-add | solution.py:143
  666.8 13.4 %scatter_custom_fusion.37 = f32[3,2432]{0,1:T(8,128)S(1)} fusion(f32[3,2432]{0,1:T(8,128)S(1)} %scatter_custom_fusion.36, s32[1664]{0:T(1024)} %copy-done.30, f32[1664]{0:T(1024)S(1)} %fusion.169, f32[1664,3]{1,0:T(8,128)S(1)} %get-tuple-element.53, f32[1664]{0:T(1024)S(1)} %sqrt.199), kind=kCustom, calls=%fused_computation.101 | custom fusion | flops 19968 | bytes 897536 | tf_op jit(solution)/shard_map/scatter-add | solution.py:145
  704.0 13.1 %scatter_custom_fusion.39 = f32[3,2432]{0,1:T(8,128)S(1)} fusion(s32[1664]{0:T(1024)} %copy-done.31, f32[]{:T(128)} %constant.17.clone.1, f32[1664]{0:T(1024)S(1)} %fusion.160, f32[1664,3]{1,0:T(8,128)S(1)} %get-tuple-element.53, f32[1664]{0:T(1024)S(1)} %sqrt.199), kind=kCustom, calls=%fused_computation.146 | custom fusion | flops 14976 | bytes 62976 | tf_op jit(solution)/shard_map/scatter-add | solution.py:143
  717.1 13.4 %scatter_custom_fusion.40 = f32[3,2432]{0,1:T(8,128)S(1)} fusion(f32[3,2432]{0,1:T(8,128)S(1)} %scatter_custom_fusion.39, s32[1664]{0:T(1024)} %copy-done.30, f32[1664]{0:T(1024)S(1)} %fusion.160, f32[1664,3]{1,0:T(8,128)S(1)} %get-tuple-element.53, f32[1664]{0:T(1024)S(1)} %sqrt.199), kind=kCustom, calls=%fused_computation.99 | custom fusion | flops 19968 | bytes 897536 | tf_op jit(solution)/shard_map/scatter-add | solution.py:145
  754.3 13.1 %scatter_custom_fusion.42 = f32[3,2432]{0,1:T(8,128)S(1)} fusion(s32[1664]{0:T(1024)} %copy-done.31, f32[]{:T(128)} %constant.17.clone.1, f32[1664]{0:T(1024)S(1)} %add_multiply_fusion.1, f32[1664,3]{1,0:T(8,128)S(1)} %get-tuple-element.53, f32[1664]{0:T(1024)S(1)} %sqrt.199), kind=kCustom, calls=%fused_computation.143 | custom fusion | flops 14976 | bytes 62976 | tf_op jit(solution)/shard_map/scatter-add | solution.py:143
  767.4 13.4 %scatter_custom_fusion.43 = f32[3,2432]{0,1:T(8,128)S(1)} fusion(f32[3,2432]{0,1:T(8,128)S(1)} %scatter_custom_fusion.42, s32[1664]{0:T(1024)} %copy-done.30, f32[1664]{0:T(1024)S(1)} %add_multiply_fusion.1, f32[1664,3]{1,0:T(8,128)S(1)} %get-tuple-element.53, f32[1664]{0:T(1024)S(1)} %sqrt.199), kind=kCustom, calls=%fused_computation.97 | custom fusion | flops 19968 | bytes 897536 | tf_op jit(solution)/shard_map/scatter-add | solution.py:145
  (403 shorter events, 371.8 us)
Async XLA Ops:
  1.3 581.0 %copy-start.44 = (s32[384]{0:T(512)}, s32[384]{0:T(512)S(1)}, u32[]{:S(2)}) copy-start(s32[384]{0:T(512)S(1)} %compare_select_fusion.2) | copy-start | bytes 4612
  7.2 4.5 collective-permute-start
  10.6 505.8 %copy-start.30 = (s32[1664]{0:T(1024)}, s32[1664]{0:T(1024)S(1)}, u32[]{:S(2)}) copy-start(s32[1664]{0:T(1024)S(1)} %get-tuple-element.69) | copy-start | bytes 19972
  75.9 3.7 collective-permute-start.1
  85.2 6.8 collective-permute-start.2
  127.9 2.7 collective-permute-start.3
  136.4 5.8 collective-permute-start.4
  178.0 2.7 collective-permute-start.5
  186.2 5.8 collective-permute-start.6
  227.9 2.7 collective-permute-start.7
  236.2 5.8 collective-permute-start.8
  277.9 2.7 collective-permute-start.9
  286.2 6.1 collective-permute-start.10
  328.1 3.3 collective-permute-start.11
  336.8 7.0 collective-permute-start.12
  379.7 2.7 collective-permute-start.13
  388.0 5.8 collective-permute-start.14
  429.6 2.7 collective-permute-start.15
  438.1 5.8 collective-permute-start.16
  479.8 2.7 collective-permute-start.17
  488.0 5.8 collective-permute-start.18
  529.7 2.7 collective-permute-start.19
  538.0 5.8 collective-permute-start.20
  579.7 2.7 collective-permute-start.21
  588.1 5.8 collective-permute-start.22
  630.1 2.7 collective-permute-start.23
  638.3 5.8 collective-permute-start.24
  680.3 2.7 collective-permute-start.25
  688.6 5.8 collective-permute-start.26
  730.5 2.7 collective-permute-start.27
  738.9 5.8 collective-permute-start.28
  780.8 2.7 collective-permute-start.29
  (44 other events, 874.2 us)
where the time goes:
time: 801 us; the launch traced here: 788 us
  other arithmetic  482 us (60%)
  local copies, waits for them, and re-layouts  179 us (22%)
  starting transfers between devices  76.3 us (10%)
  waiting for transfers between devices  47.4 us (6%)
    scatter-add x30, other arithmetic, atom_field(): force = jnp.zeros((3, count + halo), jnp.float32).at[:, first].add(weight...  395 us
    gather x24, local copies, waits for them, and re-layouts, solve_bonds(): current = current - scale * inner(unit, field[:, first] - field[:, second])  88.8 us
    ppermute x30, starting transfers between devices, shifted(): return lax.ppermute(value, axis, pairs)  76.3 us
    scatter-add x15, other arithmetic, atom_field(): own_field = inv_mass * force[:, :count].at[:, left_atoms].add(returned)  54.2 us
    ppermute x30, waiting for transfers between devices, shifted(): return lax.ppermute(value, axis, pairs)  47.4 us
    reduce_sum x19, other arithmetic, inner(): return jnp.sum(left * right, axis=0)  27.5 us
    gather x2, local copies, waits for them, and re-layouts, solve_bonds(): scale = 1.0 / jnp.sqrt(mass_ext[first] + mass_ext[second])  18.2 us
    gather x27, local copies, waits for them, and re-layouts, atom_field(): edge_field = shifted(own_field[:, left_atoms], 'dom', -1)  16.8 us
  transfers between devices with their start and end apart: 30, of which 30 were waited for; matrix products, arithmetic and copies ran while one was open for 1% of the time, Pallas kernels for 0%

commit v1 on v0

v1 whole, which is shorter than its diff:
```python
import functools
import math

import jax
import jax.numpy as jnp
from jax import lax
from jax.experimental import pallas as pl
from jax.experimental.pallas import tpu as pltpu
from jax.sharding import PartitionSpec as P

ORDER = 4
ITER = 2

time_step = 0.002
mass_oxygen = 15.9994
mass_hydrogen = 1.008
oxygen_hydrogen = 0.09572
hydrogen_pair = 0.15139
total_mass = mass_oxygen + 2.0 * mass_hydrogen
half_pair = 0.5 * hydrogen_pair
water_height = math.sqrt(oxygen_hydrogen * oxygen_hydrogen - half_pair * half_pair)
oxygen_reach = 2.0 * mass_hydrogen * water_height / total_mass
hydrogen_reach = water_height - oxygen_reach

LANES = 128
DOMAINS = 8
ATOM_ROWS = 16
BOND_ROWS = 10
SLOT_ROWS = 3
RIGHT = BOND_ROWS
LEFT = BOND_ROWS + SLOT_ROWS
CON_ROWS = BOND_ROWS + 2 * SLOT_ROWS
END_ROWS = CON_ROWS + BOND_ROWS
PLUS = LEFT * LANES

DIFF, VELO, SCAL = 0, 3 * CON_ROWS, 6 * CON_ROWS
ENDS = 7 * CON_ROWS
ATOM = ENDS + END_ROWS
POSN = ATOM + END_ROWS
MASS = POSN + END_ROWS
ROWS = MASS + END_ROWS


def lanes_of(table, index):
    dims = lax.GatherDimensionNumbers(
        offset_dims=(),
        collapsed_slice_dims=(1,),
        start_index_map=(1,),
        operand_batching_dims=(0,),
        start_indices_batching_dims=(0,),
    )
    return lax.gather(
        table, index[..., None], dims, (1, 1), mode=lax.GatherScatterMode.PROMISE_IN_BOUNDS
    )


def bits_of(row, count):
    return [(row & (1 << b)) != 0 for b in range(max(1, (count - 1).bit_length()))]


def pick(get, count, masks, low=0):
    if count == 1:
        return get(low)
    bit = (count - 1).bit_length() - 1
    half = 1 << bit
    left = pick(get, half, masks, low)
    right = pick(get, count - half, masks, low + half)
    return jnp.where(masks[bit], right, left)


def gather_rows(table, count, row, lane):
    masks = bits_of(row, count)
    return pick(lambda r: lanes_of(table(r), lane), count, masks)


def spread(ref, r):
    return jnp.broadcast_to(ref[r : r + 1, :], (8, LANES))


def place_of(position):
    lane = (position * 2521) >> 16
    return position - lane * END_ROWS, lane


def cross3(a, b):
    return [a[1] * b[2] - a[2] * b[1], a[2] * b[0] - a[0] * b[2], a[0] * b[1] - a[1] * b[0]]


def dot3(a, b):
    return a[0] * b[0] + a[1] * b[1] + a[2] * b[2]


def settle(before, after):
    old_o, old_1, old_2 = before[0:3], before[3:6], before[6:9]
    new_o, new_1, new_2 = after[0:3], after[3:6], after[6:9]
    every = range(3)
    center = [(mass_oxygen * new_o[c] + mass_hydrogen * (new_1[c] + new_2[c])) / total_mass for c in every]
    old_b = [old_1[c] - old_o[c] for c in every]
    old_c = [old_2[c] - old_o[c] for c in every]
    rel_a = [new_o[c] - center[c] for c in every]
    rel_b = [new_1[c] - center[c] for c in every]
    rel_c = [new_2[c] - center[c] for c in every]
    normal = cross3(old_b, old_c)
    side = cross3(rel_a, normal)
    upward = cross3(normal, side)

    def normed(v):
        size = jnp.sqrt(dot3(v, v))
        return [part / size for part in v]

    axis_z, axis_x, axis_y = normed(normal), normed(side), normed(upward)
    oldb_x, oldb_y = dot3(axis_x, old_b), dot3(axis_y, old_b)
    oldc_x, oldc_y = dot3(axis_x, old_c), dot3(axis_y, old_c)
    newa_z = dot3(axis_z, rel_a)
    newb_x, newb_y, newb_z = dot3(axis_x, rel_b), dot3(axis_y, rel_b), dot3(axis_z, rel_b)
    newc_x, newc_y, newc_z = dot3(axis_x, rel_c), dot3(axis_y, rel_c), dot3(axis_z, rel_c)
    sin_phi = newa_z / oxygen_reach
    cos_phi = jnp.sqrt(1.0 - sin_phi * sin_phi)
    sin_psi = (newb_z - newc_z) / (2.0 * half_pair * cos_phi)
    cos_psi = jnp.sqrt(1.0 - sin_psi * sin_psi)
    rest_ay = oxygen_reach * cos_phi
    rest_bx = -half_pair * cos_psi
    lowered = -hydrogen_reach * cos_phi
    tilted = half_pair * sin_psi * sin_phi
    rest_by = lowered - tilted
    rest_cy = lowered + tilted
    alpha = rest_bx * (oldb_x - oldc_x) + oldb_y * rest_by + oldc_y * rest_cy
    beta = rest_bx * (oldc_y - oldb_y) + oldb_x * rest_by + oldc_x * rest_cy
    gamma = oldb_x * newb_y - newb_x * oldb_y + oldc_x * newc_y - newc_x * oldc_y
    summed = alpha * alpha + beta * beta
    sin_theta = (alpha * gamma - beta * jnp.sqrt(summed - gamma * gamma)) / summed
    cos_theta = jnp.sqrt(1.0 - sin_theta * sin_theta)
    final_ax = -rest_ay * sin_theta
    final_ay = rest_ay * cos_theta
    final_bx = rest_bx * cos_theta - rest_by * sin_theta
    final_by = rest_bx * sin_theta + rest_by * cos_theta
    final_cx = -rest_bx * cos_theta - rest_cy * sin_theta
    final_cy = -rest_bx * sin_theta + rest_cy * cos_theta
    oxygen = [center[c] + axis_x[c] * final_ax + axis_y[c] * final_ay + axis_z[c] * newa_z for c in every]
    first = [center[c] + axis_x[c] * final_bx + axis_y[c] * final_by + axis_z[c] * newb_z for c in every]
    second = [center[c] + axis_x[c] * final_cx + axis_y[c] * final_cy + axis_z[c] * newc_z for c in every]
    return oxygen + first + second


def sort_keys(keys):
    lane = lax.broadcasted_iota(jnp.int32, (8, LANES), 1)
    sub = lax.broadcasted_iota(jnp.int32, (8, LANES), 0)
    base = lane * 32 + sub * 4

    def clear(bit, reg):
        if bit == 12:
            return None
        return (((base + reg) >> bit) & 1) == 0

    for size in range(1, 13):
        for bit in range(size - 1, -1, -1):
            if bit < 2:
                out = list(keys)
                for reg in range(4):
                    if reg & (1 << bit):
                        continue
                    other = reg | (1 << bit)
                    low = jnp.minimum(keys[reg], keys[other])
                    high = jnp.maximum(keys[reg], keys[other])
                    if size == 12:
                        out[reg], out[other] = low, high
                    elif size < 2:
                        up = not reg & (1 << size)
                        out[reg], out[other] = (low, high) if up else (high, low)
                    else:
                        up = clear(size, 0)
                        out[reg] = jnp.where(up, low, high)
                        out[other] = jnp.where(up, high, low)
                keys = out
                continue
            if size == 12:
                keep = ((base >> bit) & 1) == 0
            else:
                keep = (((base >> bit) ^ (base >> size)) & 1) == 0
            out = []
            for key in keys:
                if bit < 5:
                    step = 1 << (bit - 2)
                    if step == 4:
                        mate = pltpu.roll(key, 4, 0)
                    else:
                        upper = (sub & step) != 0
                        mate = jnp.where(upper, pltpu.roll(key, step, 0), pltpu.roll(key, 8 - step, 0))
                else:
                    mate = lanes_of(key, lane ^ (1 << (bit - 5)))
                out.append(jnp.where(keep, jnp.minimum(key, mate), jnp.maximum(key, mate)))
            keys = out
    return keys


def prepare(
    pos, vel, mass, bonds, left, right, water_pos, water_vel, pay, begin, water_out, atoms, ranked, ordered, wet
):
    lane = lax.broadcasted_iota(jnp.int32, (8, LANES), 1)
    sub = lax.broadcasted_iota(jnp.int32, (8, LANES), 0)

    for r in range(BOND_ROWS):
        cut = slice(r * LANES, (r + 1) * LANES)
        atoms[r : r + 1, :] = bonds[0:1, cut]
        atoms[CON_ROWS + r : CON_ROWS + r + 1, :] = bonds[1:2, cut]
    atoms[RIGHT:LEFT, :] = right[...]
    atoms[LEFT:CON_ROWS, :] = left[...]
    atoms[END_ROWS:32, :] = jnp.full((32 - END_ROWS, LANES), 2048, jnp.int32)
    ends = [atoms[8 * k : 8 * k + 8, :] for k in range(4)]
    keys = [(ends[k] * 4096 + (k * 8 + sub) * LANES + lane).astype(jnp.float32) for k in range(4)]

    done = sort_keys(keys)
    for k in range(4):
        ranked[8 * k : 8 * k + 8, :] = done[k]

    for k in range(4):
        rank = lane * END_ROWS + k * 8 + sub
        got = gather_rows(
            functools.partial(spread, ranked), 32, (rank & 3) * 8 + ((rank >> 2) & 7), rank >> 5
        ).astype(jnp.int32)
        ordered[8 * k : 8 * k + 8, :] = got
    for k in range(4):
        count = min(8, END_ROWS - 8 * k)
        got = ordered[8 * k : 8 * k + 8, :]
        end = (got & 4095).astype(jnp.float32)
        atom = jnp.minimum(got >> 12, 2047)
        weight = gather_rows(functools.partial(spread, mass), ATOM_ROWS, atom >> 7, atom & 127)
        pay[ENDS + 8 * k : ENDS + 8 * k + count, :] = end[:count]
        pay[ATOM + 8 * k : ATOM + 8 * k + count, :] = atom[:count].astype(jnp.float32)
        pay[MASS + 8 * k : MASS + 8 * k + count, :] = weight[:count]

    heads = ranked[0:1, :]
    marks = [jnp.broadcast_to(heads[:, 8 * i : 8 * i + 1], (8, LANES)) for i in range(1, 16)]
    queries = keys + [(((k * 8 + sub) * LANES + lane) * 4096).astype(jnp.float32) for k in range(2)]
    wide = jnp.broadcast_to(heads, (8, LANES))
    ranks = []
    for query in queries:
        group = jnp.zeros((8, LANES), jnp.int32)
        for mark in marks:
            group = group + jnp.where(mark <= query, 8, 0)
        column = group
        for i in range(1, 8):
            column = column + jnp.where(lanes_of(wide, group + i) <= query, 1, 0)
        rank = column * 32
        for r in range(32):
            rank = rank + jnp.where(lanes_of(spread(ranked, r), column) < query, 1, 0)
        ranks.append(rank)
    for k in range(4):
        count = min(8, END_ROWS - 8 * k)
        pay[POSN + 8 * k : POSN + 8 * k + count, :] = ranks[k][:count].astype(jnp.float32)
    for k in range(2):
        begin[8 * k : 8 * k + 8, :] = jnp.minimum(ranks[4 + k], END_ROWS * LANES - 1)

    where = [(jnp.minimum(e, 2047) >> 7, e & 127) for e in ends]

    def at_ends(table):
        return [gather_rows(table, ATOM_ROWS, row, col) for row, col in where]

    two = sub < BOND_ROWS - 8
    for base, source in ((DIFF, pos), (VELO, vel)):
        for c in range(3):
            a0, a1, b0, b1 = at_ends(
                lambda r: jnp.broadcast_to(source[c : c + 1, r * LANES : (r + 1) * LANES], (8, LANES))
            )
            pay[base + CON_ROWS * c : base + CON_ROWS * c + 8, :] = a0 - b0
            pay[base + CON_ROWS * c + 8 : base + CON_ROWS * c + 16, :] = jnp.where(two, a1 - b1, a1)
    a0, a1, b0, b1 = at_ends(functools.partial(spread, mass))
    pay[SCAL : SCAL + 8, :] = 1.0 / jnp.sqrt(a0 + b0)
    pay[SCAL + 8 : SCAL + 16, :] = jnp.where(two, 1.0 / jnp.sqrt(a1 + b1), a1)

    for j in range(8):
        cut = slice(j * LANES, (j + 1) * LANES)
        for c in range(9):
            wet[c, j : j + 1, :] = water_pos[c : c + 1, cut]
            wet[9 + c, j : j + 1, :] = water_vel[c : c + 1, cut]
    before = [wet[c] for c in range(9)]
    speed = [wet[9 + c] for c in range(9)]
    after = [before[c] + time_step * speed[c] for c in range(9)]
    settled = settle(before, after)
    for c in range(9):
        result = speed[c] + (settled[c] - after[c]) / time_step
        for j in range(8):
            water_out[c : c + 1, j * LANES : (j + 1) * LANES] = result[j : j + 1, :]


def solve(
    whole, begin, vel, out,
    con_row, con_col, end_row, end_col, atom, mass, first, second, push, unit, length, scale, diff, drift,
    now, total, field, ahead, behind, moved, more,
):
    def load(r):
        return whole[pl.ds(r, DOMAINS, stride=ROWS), :]

    def up(x):
        return pltpu.roll(x, DOMAINS - 1, 0)

    def down(x):
        return pltpu.roll(x, 1, 0)

    def before(get, v, step):
        return get(v - step) if v >= step else pltpu.roll(get(v - step + END_ROWS), 1, 1)

    def after(get, v, step):
        return get(v + step) if v + step < END_ROWS else pltpu.roll(get(v + step - END_ROWS), LANES - 1, 1)

    slots = [(RIGHT + k, LEFT + k) for k in range(SLOT_ROWS)]

    many = jnp.zeros((8, LANES), jnp.int32)
    for v in range(END_ROWS):
        end = load(ENDS + v).astype(jnp.int32)
        con = end & 2047
        con_row[v] = con >> 7
        con_col[v] = con & 127
        push[0, v] = jnp.where(end < PLUS, 1.0, -1.0)
        row, col = place_of(load(POSN + v).astype(jnp.int32))
        end_row[v] = row
        end_col[v] = col
        mass[v] = load(MASS + v)
        atom[v] = load(ATOM + v)
    for v in range(END_ROWS):
        here = atom[v]
        first[v] = jnp.where(here == before(lambda r: atom[r], v, 1), 1.0, 0.0)
        second[v] = jnp.where(here == before(lambda r: atom[r], v, 2), 1.0, 0.0)
        many = jnp.where(here == before(lambda r: atom[r], v, 4), 1, many)
    steps = jnp.where(jnp.max(many) > 0, 12, 2)

    for r in range(CON_ROWS):
        if r >= LEFT:
            continue
        d = [load(DIFF + CON_ROWS * c + r) for c in range(3)]
        g = [load(VELO + CON_ROWS * c + r) for c in range(3)]
        s = load(SCAL + r)
        if r >= RIGHT:
            other = r + SLOT_ROWS
            d = [d[c] - up(load(DIFF + CON_ROWS * c + other)) for c in range(3)]
            g = [g[c] - up(load(VELO + CON_ROWS * c + other)) for c in range(3)]
            s = 1.0 / jnp.sqrt(s + up(load(SCAL + other)))
        size = jnp.sqrt(dot3(d, d))
        part = s / size
        g = [time_step * x for x in g]
        rhs = part * dot3(d, g)
        length[r] = size
        scale[r] = s
        now[r] = rhs
        total[r] = rhs
        for c in range(3):
            diff[c, r] = d[c]
            drift[c, r] = g[c]
            unit[c, r] = part * d[c]
        if r >= RIGHT:
            now[other] = down(rhs)
            total[other] = down(rhs)
            for c in range(3):
                unit[c, other] = down(part * d[c])

    for v in range(END_ROWS):
        col = con_col[v]
        masks = bits_of(con_row[v], CON_ROWS)
        sign = push[0, v]
        parts = [pick(lambda r: lanes_of(unit[c, r], col), CON_ROWS, masks) for c in range(3)]
        for c in range(3):
            push[c, v] = sign * parts[c]
            moved[c, v] = jnp.zeros((8, LANES), jnp.float32)

    def same(ref, v):
        return ref[v] > 0.5

    def sums(source):
        for v in range(END_ROWS):
            masks = bits_of(con_row[v], CON_ROWS)
            col = con_col[v]
            x = pick(lambda r: lanes_of(source[r], col), CON_ROWS, masks)
            for c in range(3):
                field[c, v] = push[c, v] * x
        zero = jnp.zeros((8, LANES), jnp.float32)
        for c in range(3):
            one = [
                field[c, v] + jnp.where(same(first, v), before(lambda r: field[c, r], v, 1), zero)
                for v in range(END_ROWS)
            ]
            for v in range(END_ROWS):
                ahead[c, v] = one[v] + jnp.where(same(second, v), before(lambda r: one[r], v, 2), zero)
            one = [
                field[c, v]
                + jnp.where(after(lambda r: first[r], v, 1) > 0.5, after(lambda r: field[c, r], v, 1), zero)
                for v in range(END_ROWS)
            ]
            for v in range(END_ROWS):
                behind[c, v] = one[v] + jnp.where(
                    after(lambda r: second[r], v, 2) > 0.5, after(lambda r: one[r], v, 2), zero
                )

        def longer(k, carry):
            step = lax.shift_left(1, k)
            turns = step // END_ROWS
            rest = step - turns * END_ROWS

            def row(v, carry):
                here = atom[v]
                low = v - rest
                wrap = jnp.where(low < 0, 1, 0)
                low = low + wrap * END_ROWS
                shift = turns + wrap
                match = here == pltpu.roll(atom[low], shift, 1)
                high = v + rest
                wrap = jnp.where(high >= END_ROWS, 1, 0)
                high = high - wrap * END_ROWS
                back = LANES - turns - wrap
                match_back = here == pltpu.roll(atom[high], back, 1)
                for c in range(3):
                    more[c, v] = ahead[c, v] + jnp.where(match, pltpu.roll(ahead[c, low], shift, 1), 0.0)
                    more[3 + c, v] = behind[c, v] + jnp.where(
                        match_back, pltpu.roll(behind[c, high], back, 1), 0.0
                    )
                return carry

            lax.fori_loop(0, END_ROWS, row, 0)

            def keep(v, carry):
                for c in range(3):
                    ahead[c, v] = more[c, v]
                    behind[c, v] = more[3 + c, v]
                return carry

            return lax.fori_loop(0, END_ROWS, keep, carry)

        lax.fori_loop(2, steps, longer, 0)

    def apply(order, carry):
        sums(now)
        zero = jnp.zeros((8, LANES), jnp.float32)
        for v in range(END_ROWS):
            low = same(first, v)
            high = after(lambda r: first[r], v, 1) > 0.5
            rest = [
                jnp.where(low, before(lambda r: ahead[c, r], v, 1), zero)
                + jnp.where(high, after(lambda r: behind[c, r], v, 1), zero)
                for c in range(3)
            ]
            field[0, v] = mass[v] * dot3([push[c, v] for c in range(3)], rest)

        def end(v):
            masks = bits_of(end_row[v], END_ROWS)
            col = end_col[v]
            return pick(lambda r: lanes_of(field[0, r], col), END_ROWS, masks)

        for r in range(LEFT):
            if r < BOND_ROWS:
                fresh = -(end(r) + end(CON_ROWS + r))
            else:
                fresh = -(end(r) + up(end(r + SLOT_ROWS)))
                now[r + SLOT_ROWS] = down(fresh)
                total[r + SLOT_ROWS] = total[r + SLOT_ROWS] + down(fresh)
            now[r] = fresh
            total[r] = total[r] + fresh
        return carry

    def turn(index, carry):
        lax.fori_loop(0, ORDER, apply, 0)
        sums(total)
        for v in range(END_ROWS):
            for c in range(3):
                moved[c, v] = moved[c, v] + mass[v] * (ahead[c, v] + behind[c, v] - field[c, v])

        @pl.when(index < ITER)
        def _():
            def end(v):
                masks = bits_of(end_row[v], END_ROWS)
                col = end_col[v]
                return [pick(lambda r: lanes_of(moved[c, r], col), END_ROWS, masks) for c in range(3)]

            for r in range(LEFT):
                here = end(r)
                if r < BOND_ROWS:
                    there = end(CON_ROWS + r)
                else:
                    there = [up(x) for x in end(r + SLOT_ROWS)]
                g = [drift[c, r] - (here[c] - there[c]) for c in range(3)]
                excess = 2.0 * dot3([diff[c, r] for c in range(3)], g) + dot3(g, g)
                size = length[r]
                rhs = scale[r] * excess / (size + jnp.sqrt(size * size - excess))
                now[r] = rhs
                total[r] = rhs
                if r >= RIGHT:
                    now[r + SLOT_ROWS] = down(rhs)
                    total[r + SLOT_ROWS] = down(rhs)

        return carry

    lax.fori_loop(0, ITER + 1, turn, 0)

    me = lax.axis_index("dom")
    own = [
        [jnp.broadcast_to(moved[c, v, pl.ds(me, 1), :], (8, LANES)) for v in range(END_ROWS)] for c in range(3)
    ]
    names = [jnp.broadcast_to(atom[v, pl.ds(me, 1), :], (8, LANES)) for v in range(END_ROWS)]
    lane = lax.broadcasted_iota(jnp.int32, (8, LANES), 1)
    sub = lax.broadcasted_iota(jnp.int32, (8, LANES), 0)
    for k in range(2):
        row, col = place_of(begin[8 * k : 8 * k + 8, :])
        masks = bits_of(row, END_ROWS)
        name = pick(lambda r: lanes_of(names[r], col), END_ROWS, masks).astype(jnp.int32)
        bound = name == (k * 8 + sub) * LANES + lane
        for c in range(3):
            shift = pick(lambda r: lanes_of(own[c][r], col), END_ROWS, masks)
            shift = jnp.where(bound, shift, 0.0) / time_step
            for j in range(8):
                cut = slice((8 * k + j) * LANES, (8 * k + j + 1) * LANES)
                out[c : c + 1, cut] = vel[c : c + 1, cut] - shift[j : j + 1, :]


def on_device(
    protein_pos, protein_vel, inv_mass, bond_atoms, left_atoms, right_atoms, water_pos, water_vel
):
    f32, i32 = jnp.float32, jnp.int32
    mass = inv_mass.reshape(ATOM_ROWS, LANES)
    pay, begin, water_velocity = pl.pallas_call(
        prepare,
        out_shape=(
            jax.ShapeDtypeStruct((ROWS, LANES), f32),
            jax.ShapeDtypeStruct((ATOM_ROWS, LANES), i32),
            jax.ShapeDtypeStruct(water_pos.shape, f32),
        ),
        scratch_shapes=[
            pltpu.VMEM((32, LANES), i32),
            pltpu.VMEM((32, LANES), f32),
            pltpu.VMEM((32, LANES), i32),
            pltpu.VMEM((18, 8, LANES), f32),
        ],
        name="prepare",
    )(
        protein_pos,
        protein_vel,
        mass,
        bond_atoms,
        left_atoms.reshape(SLOT_ROWS, LANES),
        right_atoms.reshape(SLOT_ROWS, LANES),
        water_pos,
        water_vel,
    )
    whole = lax.all_gather(pay, "dom", axis=0, tiled=True)

    def block(*lead, dtype=f32):
        return pltpu.VMEM((*lead, 8, LANES), dtype)

    protein_velocity = pl.pallas_call(
        solve,
        out_shape=jax.ShapeDtypeStruct(protein_vel.shape, f32),
        scratch_shapes=[
            block(END_ROWS, dtype=i32),
            block(END_ROWS, dtype=i32),
            block(END_ROWS, dtype=i32),
            block(END_ROWS, dtype=i32),
            block(END_ROWS),
            block(END_ROWS),
            block(END_ROWS),
            block(END_ROWS),
            block(3, END_ROWS),
            block(3, CON_ROWS),
            block(CON_ROWS),
            block(CON_ROWS),
            block(3, CON_ROWS),
            block(3, CON_ROWS),
            block(CON_ROWS),
            block(CON_ROWS),
            block(3, END_ROWS),
            block(3, END_ROWS),
            block(3, END_ROWS),
            block(3, END_ROWS),
            block(6, END_ROWS),
        ],
        name="solve",
    )(whole, begin, protein_vel)
    return (protein_velocity, water_velocity)


def solution(mesh):
    in_specs = (
        P(None, ("rep", "dom")),
        P(None, ("rep", "dom")),
        P(("rep", "dom")),
        P(None, ("rep", "dom")),
        P(("rep", "dom")),
        P(("rep", "dom")),
        P(None, ("rep", "dom")),
        P(None, ("rep", "dom")),
    )
    out_specs = (P(None, ("rep", "dom")), P(None, ("rep", "dom")))
    return jax.shard_map(
        on_device, mesh=mesh, in_specs=in_specs, out_specs=out_specs, check_vma=False
    )
```

time: 801 us -> 55.4 us (0.07); the launches traced: 788 us -> 55.2 us
  other arithmetic: 482 us -> 0 us
  local copies, waits for them, and re-layouts: 179 us -> 0 us
  starting transfers between devices: 76.3 us -> 0 us
  waiting for transfers between devices: 47.4 us -> 0 us
  Pallas kernels: 0 us -> 34.8 us
  blocking collectives: 0 us -> 19.8 us
    scatter-add x45 -> x0, other arithmetic: 449 us -> none  [the longest x30 395 us: atom_field(): force = jnp.zeros((3, count + halo), jnp.float32).at[:, first].add(weight...]
    gather x66 -> x0, local copies, waits for them, and re-layouts: 160 us -> none  [the longest x24 88.8 us: solve_bonds(): current = current - scale * inner(unit, field[:, first] - field[:, second])]
    ppermute x30 -> x0, starting transfers between devices: 76.3 us -> none  [shifted(): return lax.ppermute(value, axis, pairs)]
    ppermute x30 -> x0, waiting for transfers between devices: 47.4 us -> none  [shifted(): return lax.ppermute(value, axis, pairs)]
    pallas_call x0 -> x2, Pallas kernels: none -> 34.8 us  [the longest x1 30.2 us: on_device(): pl.pallas_call(solve, out_shape=jax.ShapeDtypeStruct(protein_vel.shape, f...]
    reduce_sum x19 -> x0, other arithmetic: 27.5 us -> none  [inner(): return jnp.sum(left * right, axis=0)]
    all_gather x0 -> x1, blocking collectives: none -> 19.8 us  [on_device(): whole = lax.all_gather(pay, 'dom', axis=0, tiled=True)]
  transfers between devices with their start and end apart: 30 -> 0, of which waited for: 30 -> 0; matrix products, arithmetic and copies ran while one was open for 1% -> 0% of each run, Pallas kernels for 0% -> 0%
where the time goes in v1:
time: 55.4 us; the launch traced here: 55.2 us
  Pallas kernels  34.8 us (63%)
  blocking collectives  19.8 us (36%)
  between operations  0.63 us (1%)
    pallas_call x1, Pallas kernels, on_device(): pl.pallas_call(solve, out_shape=jax.ShapeDtypeStruct(protein_vel.shape, f...  30.2 us
    all_gather x1, blocking collectives, on_device(): whole = lax.all_gather(pay, 'dom', axis=0, tiled=True)  19.8 us
    pallas_call x1, Pallas kernels, on_device(): pl.pallas_call(prepare, out_shape=(jax.ShapeDtypeStruct((ROWS, LANES), f3...  4.61 us

profile of v1, /device:TPU:1, one launch (start us, length us, event | category | flops | bytes accessed | tf_op | source)
XLA Modules:
  0.0 55.2 jit_solution(6663413001107262234)
XLA Ops:
  0.6 4.6 %prepare.1 = (f32[216,128]{1,0:T(8,128)}, s32[16,128]{1,0:T(8,128)}, f32[9,1024]{1,0:T(8,128)}) custom-call(f32[3,2048]{1,0:T(4,128)} %pos.1, f32[3,2048]{1,0:T(4,128)} %vel.3, f32[16,128]{1,0:T(8,128)} %bitcast.3, s32[2,1280]{1,0:T(2,128)} %bonds.1, s32[3,128]{1,0:T(4,128)} %bitcast.4, s32[3,128]{1,0:T(4,128)} %bitcast.5, f32[9,1024]{1,0:T(8,128)} %water_pos.1, ...), custom_call_target="tpu_custom_call" | custom-call | tf_op jit(solution)/shard_map/prepare/pallas_call | solution.py:517
  5.2 19.8 %all_gather.3.whole = f32[1728,128]{1,0:T(8,128)} all-gather(f32[216,128]{1,0:T(8,128)} %get-tuple-element.5), channel_id=1, replica_groups=mesh['rep'=32,'dom'=8] {'dom'}, dimensions={0}, use_global_device_ids=true | all-gather | bytes 995328 | tf_op jit(solution)/shard_map/all_gather | solution.py:541
  25.0 30.2 %solve.1 = f32[3,2048]{1,0:T(4,128)} custom-call(f32[1728,128]{1,0:T(8,128)} %all_gather.3.whole, s32[16,128]{1,0:T(8,128)} %get-tuple-element.6.begin, f32[3,2048]{1,0:T(4,128)} %vel.3), custom_call_target="tpu_custom_call" | custom-call | tf_op jit(solution)/shard_map/solve/pallas_call | solution.py:546

commit v2 on v0

v2 whole, which is shorter than its diff:
```python
import functools
import math

import jax
import jax.numpy as jnp
from jax import lax
from jax.experimental import pallas as pl
from jax.experimental.pallas import tpu as pltpu
from jax.sharding import PartitionSpec as P

ORDER = 4
ITER = 2

time_step = 0.002
mass_oxygen = 15.9994
mass_hydrogen = 1.008
oxygen_hydrogen = 0.09572
hydrogen_pair = 0.15139
total_mass = mass_oxygen + 2.0 * mass_hydrogen
half_pair = 0.5 * hydrogen_pair
water_height = math.sqrt(oxygen_hydrogen * oxygen_hydrogen - half_pair * half_pair)
oxygen_reach = 2.0 * mass_hydrogen * water_height / total_mass
hydrogen_reach = water_height - oxygen_reach

LANES = 128
DOMAINS = 8
ATOM_ROWS = 16
BOND_ROWS = 10
SLOT_ROWS = 3
END_ROWS = 2 * BOND_ROWS
CROSS_ROWS = 2 * SLOT_ROWS
HALF = BOND_ROWS * LANES
NEAR = 3
NONE = 4095

DIFF, VELO, SCAL = 0, 3 * END_ROWS, 6 * END_ROWS
MASS, ATOM, MATE, LINK = (k * END_ROWS for k in (7, 8, 9, 10))
CPOS = 11 * END_ROWS
CVEL, CMAS, HOST = CPOS + 3 * CROSS_ROWS, CPOS + 6 * CROSS_ROWS, CPOS + 7 * CROSS_ROWS
ROWS = -(-(CPOS + 8 * CROSS_ROWS) // 8) * 8


def lanes_of(table, index):
    dims = lax.GatherDimensionNumbers(
        offset_dims=(),
        collapsed_slice_dims=(1,),
        start_index_map=(1,),
        operand_batching_dims=(0,),
        start_indices_batching_dims=(0,),
    )
    return lax.gather(
        table, index[..., None], dims, (1, 1), mode=lax.GatherScatterMode.PROMISE_IN_BOUNDS
    )


def bits_of(row, count):
    return [(row & (1 << b)) != 0 for b in range(max(1, (count - 1).bit_length()))]


def pick(get, count, masks, low=0):
    if count == 1:
        return get(low)
    bit = (count - 1).bit_length() - 1
    half = 1 << bit
    left = pick(get, half, masks, low)
    right = pick(get, count - half, masks, low + half)
    return jnp.where(masks[bit], right, left)


def gather_rows(table, count, row, lane):
    masks = bits_of(row, count)
    return pick(lambda r: lanes_of(table(r), lane), count, masks)


def spread(ref, r):
    return jnp.broadcast_to(ref[r : r + 1, :], (8, LANES))


def place_of(position):
    lane = (position * 3277) >> 16
    return position - lane * END_ROWS, lane


def cross3(a, b):
    return [a[1] * b[2] - a[2] * b[1], a[2] * b[0] - a[0] * b[2], a[0] * b[1] - a[1] * b[0]]


def dot3(a, b):
    return a[0] * b[0] + a[1] * b[1] + a[2] * b[2]


def settle(before, after):
    old_o, old_1, old_2 = before[0:3], before[3:6], before[6:9]
    new_o, new_1, new_2 = after[0:3], after[3:6], after[6:9]
    every = range(3)
    center = [(mass_oxygen * new_o[c] + mass_hydrogen * (new_1[c] + new_2[c])) / total_mass for c in every]
    old_b = [old_1[c] - old_o[c] for c in every]
    old_c = [old_2[c] - old_o[c] for c in every]
    rel_a = [new_o[c] - center[c] for c in every]
    rel_b = [new_1[c] - center[c] for c in every]
    rel_c = [new_2[c] - center[c] for c in every]
    normal = cross3(old_b, old_c)
    side = cross3(rel_a, normal)
    upward = cross3(normal, side)

    def normed(v):
        size = jnp.sqrt(dot3(v, v))
        return [part / size for part in v]

    axis_z, axis_x, axis_y = normed(normal), normed(side), normed(upward)
    oldb_x, oldb_y = dot3(axis_x, old_b), dot3(axis_y, old_b)
    oldc_x, oldc_y = dot3(axis_x, old_c), dot3(axis_y, old_c)
    newa_z = dot3(axis_z, rel_a)
    newb_x, newb_y, newb_z = dot3(axis_x, rel_b), dot3(axis_y, rel_b), dot3(axis_z, rel_b)
    newc_x, newc_y, newc_z = dot3(axis_x, rel_c), dot3(axis_y, rel_c), dot3(axis_z, rel_c)
    sin_phi = newa_z / oxygen_reach
    cos_phi = jnp.sqrt(1.0 - sin_phi * sin_phi)
    sin_psi = (newb_z - newc_z) / (2.0 * half_pair * cos_phi)
    cos_psi = jnp.sqrt(1.0 - sin_psi * sin_psi)
    rest_ay = oxygen_reach * cos_phi
    rest_bx = -half_pair * cos_psi
    lowered = -hydrogen_reach * cos_phi
    tilted = half_pair * sin_psi * sin_phi
    rest_by = lowered - tilted
    rest_cy = lowered + tilted
    alpha = rest_bx * (oldb_x - oldc_x) + oldb_y * rest_by + oldc_y * rest_cy
    beta = rest_bx * (oldc_y - oldb_y) + oldb_x * rest_by + oldc_x * rest_cy
    gamma = oldb_x * newb_y - newb_x * oldb_y + oldc_x * newc_y - newc_x * oldc_y
    summed = alpha * alpha + beta * beta
    sin_theta = (alpha * gamma - beta * jnp.sqrt(summed - gamma * gamma)) / summed
    cos_theta = jnp.sqrt(1.0 - sin_theta * sin_theta)
    final_ax = -rest_ay * sin_theta
    final_ay = rest_ay * cos_theta
    final_bx = rest_bx * cos_theta - rest_by * sin_theta
    final_by = rest_bx * sin_theta + rest_by * cos_theta
    final_cx = -rest_bx * cos_theta - rest_cy * sin_theta
    final_cy = -rest_bx * sin_theta + rest_cy * cos_theta
    oxygen = [center[c] + axis_x[c] * final_ax + axis_y[c] * final_ay + axis_z[c] * newa_z for c in every]
    first = [center[c] + axis_x[c] * final_bx + axis_y[c] * final_by + axis_z[c] * newb_z for c in every]
    second = [center[c] + axis_x[c] * final_cx + axis_y[c] * final_cy + axis_z[c] * newc_z for c in every]
    return oxygen + first + second


def sort_keys(keys):
    lane = lax.broadcasted_iota(jnp.int32, (8, LANES), 1)
    sub = lax.broadcasted_iota(jnp.int32, (8, LANES), 0)
    reg_bits = (len(keys) - 1).bit_length()
    bits = reg_bits + 10
    base = (lane * 8 + sub) << reg_bits

    for size in range(1, bits + 1):
        for bit in range(size - 1, -1, -1):
            if bit < reg_bits:
                out = list(keys)
                for reg in range(len(keys)):
                    if reg & (1 << bit):
                        continue
                    other = reg | (1 << bit)
                    low = jnp.minimum(keys[reg], keys[other])
                    high = jnp.maximum(keys[reg], keys[other])
                    if size == bits:
                        out[reg], out[other] = low, high
                    elif size < reg_bits:
                        out[reg], out[other] = (high, low) if reg & (1 << size) else (low, high)
                    else:
                        rising = ((base >> size) & 1) == 0
                        out[reg] = jnp.where(rising, low, high)
                        out[other] = jnp.where(rising, high, low)
                keys = out
                continue
            turned = base >> bit if size == bits else (base >> bit) ^ (base >> size)
            keep = (turned & 1) == 0
            out = []
            for key in keys:
                step = 1 << (bit - reg_bits)
                if step == 4:
                    mate = pltpu.roll(key, 4, 0)
                elif step < 4:
                    upper = (sub & step) != 0
                    mate = jnp.where(upper, pltpu.roll(key, step, 0), pltpu.roll(key, 8 - step, 0))
                else:
                    mate = lanes_of(key, lane ^ (step // 8))
                out.append(jnp.where(keep, jnp.minimum(key, mate), jnp.maximum(key, mate)))
            keys = out
    return keys


def find(table, rows, queries):
    heads = table[0:1, :]
    marks = [jnp.broadcast_to(heads[:, 8 * i : 8 * i + 1], (8, LANES)) for i in range(1, 16)]
    wide = jnp.broadcast_to(heads, (8, LANES))
    found = []
    for query in queries:
        group = jnp.zeros((8, LANES), jnp.int32)
        for mark in marks:
            group = group + jnp.where(mark < query, 8, 0)
        column = group
        for i in range(1, 8):
            column = column + jnp.where(lanes_of(wide, group + i) < query, 1, 0)
        rank = column * rows
        best = jnp.full((8, LANES), -1.0, jnp.float32)
        for r in range(rows):
            key = lanes_of(spread(table, r), column)
            below = key < query
            rank = rank + jnp.where(below, 1, 0)
            best = jnp.maximum(best, jnp.where(below, key, -1.0))
        found.append((rank, best.astype(jnp.int32)))
    return found


def prepare(
    pos, vel, mass, bonds, left, right, water_pos, water_vel, pay, place, water_out, atoms, ranked, slots, wet
):
    lane = lax.broadcasted_iota(jnp.int32, (8, LANES), 1)
    sub = lax.broadcasted_iota(jnp.int32, (8, LANES), 0)
    f32, i32 = jnp.float32, jnp.int32

    def index(k):
        return (k * 8 + sub) * LANES + lane

    for r in range(BOND_ROWS):
        cut = slice(r * LANES, (r + 1) * LANES)
        atoms[r : r + 1, :] = bonds[0:1, cut]
        atoms[BOND_ROWS + r : BOND_ROWS + r + 1, :] = bonds[1:2, cut]
    atoms[END_ROWS:32, :] = jnp.full((32 - END_ROWS, LANES), 2048, i32)
    atoms[32 : 32 + SLOT_ROWS, :] = right[...]
    atoms[32 + SLOT_ROWS : 32 + CROSS_ROWS, :] = left[...]
    atoms[32 + CROSS_ROWS : 40, :] = jnp.full((8 - CROSS_ROWS, LANES), 4096, i32)
    crossed = atoms[32:40, :]

    keys = [(atoms[8 * k : 8 * k + 8, :] * 4096 + index(k)).astype(f32) for k in range(4)]
    keys = sort_keys(keys)
    for k in range(4):
        ranked[8 * k : 8 * k + 8, :] = keys[k]
    slots[...] = sort_keys([(crossed * 1024 + index(0)).astype(f32)])[0]

    own, far, mates = [], [], []
    for k in range(3):
        rank = lane * END_ROWS + k * 8 + sub
        key = gather_rows(
            functools.partial(spread, ranked), 32, (rank & 3) * 8 + ((rank >> 2) & 7), rank >> 5
        ).astype(i32)
        end = key & 4095
        mate = jnp.where(end < HALF, end + HALF, end - HALF)
        other = gather_rows(functools.partial(spread, atoms), END_ROWS, mate >> 7, mate & 127)
        own.append(jnp.minimum(key >> 12, 2047))
        far.append(jnp.minimum(other, 2047))
        mates.append((other * 4096 + mate).astype(f32))

    def put(block, k, value):
        count = min(8, END_ROWS - 8 * k)
        pay[block + 8 * k : block + 8 * k + count, :] = value[:count].astype(f32)

    inside = find(
        ranked,
        32,
        mates + [((crossed + 1) * 4096).astype(f32)] + [((index(k) + 1) * 4096).astype(f32) for k in range(2)],
    )
    outside = find(
        slots, 8, [((a + 1) * 1024).astype(f32) for a in own] + [((index(k) + 1) * 1024).astype(f32) for k in range(2)]
    )
    for k in range(3):
        put(ATOM, k, own[k])
        put(MATE, k, inside[k][0])
        best = outside[k][1]
        put(LINK, k, jnp.where(best >> 10 == own[k], best & 1023, NONE))
    rank, best = inside[3]
    host = jnp.where(best >> 12 == crossed, rank - 1, NONE)
    pay[HOST : HOST + CROSS_ROWS, :] = host[:CROSS_ROWS].astype(f32)
    for k in range(2):
        rank, best = inside[4 + k]
        slot = outside[3 + k][1]
        row, col = place_of(rank - 1)
        place[8 * k : 8 * k + 8, :] = jnp.where(
            best >> 12 == index(k),
            row * LANES + col,
            jnp.where(slot >> 10 == index(k), END_ROWS * LANES + (slot & 1023), -1),
        )

    edge = jnp.minimum(crossed, 2047)
    where = [(a >> 7, a & 127) for a in own + far + [edge]]

    def at_ends(table):
        return [gather_rows(table, ATOM_ROWS, row, col) for row, col in where]

    for block, cross, source in ((DIFF, CPOS, pos), (VELO, CVEL, vel)):
        for c in range(3):
            values = at_ends(
                lambda r: jnp.broadcast_to(source[c : c + 1, r * LANES : (r + 1) * LANES], (8, LANES))
            )
            for k in range(3):
                put(block + END_ROWS * c, k, values[k] - values[3 + k])
            pay[cross + CROSS_ROWS * c : cross + CROSS_ROWS * (c + 1), :] = values[6][:CROSS_ROWS]
    values = at_ends(functools.partial(spread, mass))
    for k in range(3):
        put(MASS, k, values[k])
        put(SCAL, k, 1.0 / jnp.sqrt(values[k] + values[3 + k]))
    pay[CMAS : CMAS + CROSS_ROWS, :] = values[6][:CROSS_ROWS]

    for j in range(8):
        cut = slice(j * LANES, (j + 1) * LANES)
        for c in range(9):
            wet[c, j : j + 1, :] = water_pos[c : c + 1, cut]
            wet[9 + c, j : j + 1, :] = water_vel[c : c + 1, cut]
    before = [wet[c] for c in range(9)]
    speed = [wet[9 + c] for c in range(9)]
    after = [before[c] + time_step * speed[c] for c in range(9)]
    settled = settle(before, after)
    for c in range(9):
        result = speed[c] + (settled[c] - after[c]) / time_step
        for j in range(8):
            water_out[c : c + 1, j * LANES : (j + 1) * LANES] = result[j : j + 1, :]


def solve(
    whole, place, vel, out,
    mate_row, mate_col, link_row, link_col, host_row, host_col, atom, mass, push, length, scale, diff, drift,
    below, above, near, hinge, edge, edge_mass, edge_length, edge_scale, edge_diff, edge_drift, anchor,
    now, total, now_edge, total_edge, part, ties, moved, moved_edge, run, more,
):
    zero = jnp.zeros((8, LANES), jnp.float32)
    every, ends, right = range(3), range(END_ROWS), range(SLOT_ROWS)

    def load(r):
        return whole[pl.ds(r, DOMAINS, stride=ROWS), :]

    def up(x):
        return pltpu.roll(x, DOMAINS - 1, 0)

    def down(x):
        return pltpu.roll(x, 1, 0)

    def around(rows):
        wide = {v: rows[v] for v in ends}
        for s in range(1, NEAR + 1):
            wide[-s] = pltpu.roll(rows[END_ROWS - s], 1, 1)
            wide[END_ROWS - 1 + s] = pltpu.roll(rows[s - 1], LANES - 1, 1)
        return wide

    def choose(rows, count, masks, col):
        return pick(lambda r: lanes_of(rows[r], col), count, masks)

    def both(values):
        return values + [down(x) for x in values]

    for v in ends:
        row, col = place_of(load(MATE + v).astype(jnp.int32))
        mate_row[v], mate_col[v] = row, col
        slot = load(LINK + v).astype(jnp.int32)
        link_row[v], link_col[v] = slot >> 7, slot & 127
        mass[v] = load(MASS + v)
        atom[v] = load(ATOM + v)
    for r in range(CROSS_ROWS):
        row, col = place_of(load(HOST + r).astype(jnp.int32))
        host_row[r], host_col[r] = row, jnp.minimum(col, LANES - 1)
        anchor[r] = jnp.where(col < LANES, 1.0, 0.0)

    for v in ends:
        d = [load(DIFF + END_ROWS * c + v) for c in every]
        g = [time_step * load(VELO + END_ROWS * c + v) for c in every]
        s = load(SCAL + v)
        size = jnp.sqrt(dot3(d, d))
        rate = s / size
        rhs = rate * dot3(d, g)
        length[v], scale[v], now[v], total[v] = size, s, rhs, rhs
        for c in every:
            diff[c, v], drift[c, v], push[c, v], moved[c, v] = d[c], g[c], rate * d[c], zero

    start = []
    for r in right:
        l = r + SLOT_ROWS
        d = [load(CPOS + CROSS_ROWS * c + r) - up(load(CPOS + CROSS_ROWS * c + l)) for c in every]
        g = [
            time_step * (load(CVEL + CROSS_ROWS * c + r) - up(load(CVEL + CROSS_ROWS * c + l))) for c in every
        ]
        edge_mass[r], edge_mass[l] = load(CMAS + r), load(CMAS + l)
        s = 1.0 / jnp.sqrt(edge_mass[r] + up(edge_mass[l]))
        size = jnp.sqrt(dot3(d, d))
        rate = s / size
        edge_length[r], edge_scale[r] = size, s
        start.append(rate * dot3(d, g))
        for c in every:
            edge_diff[c, r], edge_drift[c, r] = d[c], g[c]
            edge[c, r], edge[c, l] = rate * d[c], -down(rate * d[c])
            moved_edge[c, r], moved_edge[c, l] = zero, zero
    for r, x in enumerate(both(start)):
        now_edge[r], total_edge[r] = x, x

    names = around([atom[v] for v in ends])
    many = jnp.zeros((8, LANES), jnp.int32)
    fields = [around([push[c, v] for v in ends]) for c in every]
    for v in ends:
        here = [mass[v] * push[c, v] for c in every]
        for s in range(1, NEAR + 1):
            same = names[v] == names[v - s]
            near[s - 1, v] = jnp.where(same, 1.0, 0.0)
            below[s - 1, v] = jnp.where(same, dot3(here, [fields[c][v - s] for c in every]), 0.0)
            above[s - 1, v] = jnp.where(
                names[v] == names[v + s], dot3(here, [fields[c][v + s] for c in every]), 0.0
            )
        past = names[v - 4] if v >= 1 else pltpu.roll(atom[END_ROWS - 4], 1, 1)
        many = jnp.where(names[v] == past, 1, many)
        masks = bits_of(link_row[v], CROSS_ROWS)
        linked = link_row[v] < CROSS_ROWS
        across = [choose([edge[c, r] for r in range(CROSS_ROWS)], CROSS_ROWS, masks, link_col[v]) for c in every]
        for c in every:
            ties[c, v] = jnp.where(linked, mass[v] * across[c], 0.0)
        hinge[v] = jnp.where(linked, dot3(here, across), 0.0)
    crowded = jnp.max(many) > 0

    def gated(factor, value):
        return jnp.where(factor != 0.0, factor * value, 0.0)

    def scan(rows, forward):
        def double(k, carry):
            step = lax.shift_left(1, k)
            turns = step // END_ROWS
            rest = step - turns * END_ROWS

            def one(v, carry):
                source = v - rest if forward else v + rest
                wrap = jnp.where(source < 0, 1, 0) if forward else jnp.where(source >= END_ROWS, 1, 0)
                source = source + wrap * END_ROWS if forward else source - wrap * END_ROWS
                shift = turns + wrap if forward else (LANES - turns - wrap)
                match = atom[v] == pltpu.roll(atom[source], shift, 1)
                for r in rows:
                    more[r, v] = run[r, v] + jnp.where(match, pltpu.roll(run[r, source], shift, 1), 0.0)
                return carry

            lax.fori_loop(0, END_ROWS, one, 0)

            def keep(v, carry):
                for r in rows:
                    run[r, v] = more[r, v]
                return carry

            return lax.fori_loop(0, END_ROWS, keep, carry)

        lax.fori_loop(0, 12, double, 0)

    def scan_fields(source):
        def fill(v, carry):
            x = source[v]
            for c in every:
                run[c, v] = push[c, v] * x
                run[3 + c, v] = push[c, v] * x
            run[6, v] = gated(hinge[v], x)
            return carry

        lax.fori_loop(0, END_ROWS, fill, 0)
        scan((0, 1, 2, 6), True)
        scan((3, 4, 5), False)

    def at_edges(table):
        got = []
        for r in range(CROSS_ROWS):
            value = choose(table, END_ROWS, bits_of(host_row[r], END_ROWS), host_col[r])
            got.append(value)
        return got

    def apply(order, carry):
        x = around([now[v] for v in ends])
        bound = {v: gated(hinge[v], x[v]) for v in ends}
        wide = around([bound[v] for v in ends])
        for v in ends:
            sum_x, sum_bound = zero, bound[v]
            for s in range(1, NEAR + 1):
                sum_x = sum_x + gated(below[s - 1, v], x[v - s])
                sum_x = sum_x + gated(above[s - 1, v], x[v + s])
                sum_bound = sum_bound + jnp.where(near[s - 1, v] > 0.5, wide[v - s], 0.0)
            part[0, v] = sum_x
            part[1, v] = sum_bound

        @pl.when(crowded)
        def _():
            scan_fields(now)

            def fill(v, carry):
                here = [push[c, v] for c in every]
                both_sides = [run[c, v] + run[3 + c, v] - 2.0 * here[c] * now[v] for c in every]
                part[0, v] = mass[v] * dot3(here, both_sides)
                part[1, v] = run[6, v]
                return carry

            lax.fori_loop(0, END_ROWS, fill, 0)

        crossing = [now_edge[r] for r in range(CROSS_ROWS)]
        whole_part = []
        for v in ends:
            value = choose(crossing, CROSS_ROWS, bits_of(link_row[v], CROSS_ROWS), link_col[v])
            whole_part.append(part[0, v] + gated(hinge[v], value))
        pulled = at_edges([part[1, v] for v in ends])
        pulled = [jnp.where(anchor[r] > 0.5, pulled[r], 0.0) for r in range(CROSS_ROWS)]
        for r, value in enumerate(both([-(pulled[r] + up(pulled[r + SLOT_ROWS])) for r in right])):
            now_edge[r] = value
            total_edge[r] = total_edge[r] + value
        for v in ends:
            value = choose(whole_part, END_ROWS, bits_of(mate_row[v], END_ROWS), mate_col[v])
            value = -(whole_part[v] + value)
            now[v] = value
            total[v] = total[v] + value
        return carry

    def edges_moved():
        got = []
        for r in range(CROSS_ROWS):
            masks = bits_of(host_row[r], END_ROWS)
            fast = anchor[r] > 0.5
            got.append(
                [
                    jnp.where(fast, choose([moved[c, v] for v in ends], END_ROWS, masks, host_col[r]), moved_edge[c, r])
                    for c in every
                ]
            )
        return got

    def turn(index, carry):
        lax.fori_loop(0, ORDER, apply, 0)

        x = [total[v] for v in ends]
        for c in every:
            field = around([push[c, v] * x[v] for v in ends])
            for v in ends:
                value = field[v]
                for s in range(1, NEAR + 1):
                    value = value + jnp.where(names_equal(v, -s), field[v - s], 0.0)
                    value = value + jnp.where(names_equal(v, s), field[v + s], 0.0)
                run[c, v] = value

        @pl.when(crowded)
        def _():
            scan_fields(total)

            def fill(v, carry):
                for c in every:
                    run[c, v] = run[c, v] + run[3 + c, v] - push[c, v] * total[v]
                return carry

            lax.fori_loop(0, END_ROWS, fill, 0)

        crossing = [total_edge[r] for r in range(CROSS_ROWS)]
        for v in ends:
            value = choose(crossing, CROSS_ROWS, bits_of(link_row[v], CROSS_ROWS), link_col[v])
            linked = link_row[v] < CROSS_ROWS
            for c in every:
                moved[c, v] = moved[c, v] + mass[v] * run[c, v] + jnp.where(linked, ties[c, v] * value, 0.0)
        for r in range(CROSS_ROWS):
            for c in every:
                moved_edge[c, r] = moved_edge[c, r] + edge_mass[r] * edge[c, r] * crossing[r]

        def correct(d, g, size, s):
            excess = 2.0 * dot3(d, g) + dot3(g, g)
            return s * excess / (size + jnp.sqrt(size * size - excess))

        @pl.when(index < ITER)
        def _():
            here = edges_moved()
            start = []
            for r in right:
                g = [edge_drift[c, r] - (here[r][c] - up(here[r + SLOT_ROWS][c])) for c in every]
                start.append(correct([edge_diff[c, r] for c in every], g, edge_length[r], edge_scale[r]))
            for r, value in enumerate(both(start)):
                now_edge[r], total_edge[r] = value, value
            for v in ends:
                masks = bits_of(mate_row[v], END_ROWS)
                there = [choose([moved[c, w] for w in ends], END_ROWS, masks, mate_col[v]) for c in every]
                g = [drift[c, v] - (moved[c, v] - there[c]) for c in every]
                value = correct([diff[c, v] for c in every], g, length[v], scale[v])
                now[v], total[v] = value, value

        return carry

    def names_equal(v, s):
        flag = near[s - 1, v + s] if s > 0 and v + s < END_ROWS else None
        if s < 0:
            flag = near[-s - 1, v]
        elif flag is None:
            flag = pltpu.roll(near[s - 1, v + s - END_ROWS], LANES - 1, 1)
        return flag > 0.5

    lax.fori_loop(0, ITER + 1, turn, 0)

    me = lax.axis_index("dom")
    edges = edges_moved()
    for r in range(CROSS_ROWS):
        for c in every:
            moved_edge[c, r] = edges[r][c]
    own = [
        [jnp.broadcast_to(moved[c, v, pl.ds(me, 1), :], (8, LANES)) for v in ends]
        + [jnp.broadcast_to(moved_edge[c, r, pl.ds(me, 1), :], (8, LANES)) for r in range(CROSS_ROWS)]
        for c in every
    ]
    for k in range(2):
        code = place[8 * k : 8 * k + 8, :]
        bound = code >= 0
        code = jnp.maximum(code, 0)
        masks = bits_of(code >> 7, END_ROWS + CROSS_ROWS)
        for c in every:
            shift = choose(own[c], END_ROWS + CROSS_ROWS, masks, code & 127)
            shift = jnp.where(bound, shift, 0.0) / time_step
            for j in range(8):
                cut = slice((8 * k + j) * LANES, (8 * k + j + 1) * LANES)
                out[c : c + 1, cut] = vel[c : c + 1, cut] - shift[j : j + 1, :]


def on_device(
    protein_pos, protein_vel, inv_mass, bond_atoms, left_atoms, right_atoms, water_pos, water_vel
):
    f32, i32 = jnp.float32, jnp.int32
    mass = inv_mass.reshape(ATOM_ROWS, LANES)
    pay, place, water_velocity = pl.pallas_call(
        prepare,
        out_shape=(
            jax.ShapeDtypeStruct((ROWS, LANES), f32),
            jax.ShapeDtypeStruct((ATOM_ROWS, LANES), i32),
            jax.ShapeDtypeStruct(water_pos.shape, f32),
        ),
        scratch_shapes=[
            pltpu.VMEM((40, LANES), i32),
            pltpu.VMEM((32, LANES), f32),
            pltpu.VMEM((8, LANES), f32),
            pltpu.VMEM((18, 8, LANES), f32),
        ],
        name="prepare",
    )(
        protein_pos,
        protein_vel,
        mass,
        bond_atoms,
        left_atoms.reshape(SLOT_ROWS, LANES),
        right_atoms.reshape(SLOT_ROWS, LANES),
        water_pos,
        water_vel,
    )
    whole = lax.all_gather(pay, "dom", axis=0, tiled=True)

    def rows(*lead, dtype=f32):
        return pltpu.VMEM((*lead, 8, LANES), dtype)

    n, m = END_ROWS, CROSS_ROWS
    protein_velocity = pl.pallas_call(
        solve,
        out_shape=jax.ShapeDtypeStruct(protein_vel.shape, f32),
        scratch_shapes=[
            *(rows(n, dtype=i32) for _ in range(4)),
            *(rows(m, dtype=i32) for _ in range(2)),
            *(rows(n) for _ in range(2)),
            rows(3, n),
            *(rows(n) for _ in range(2)),
            *(rows(3, n) for _ in range(2)),
            *(rows(NEAR, n) for _ in range(3)),
            rows(n),
            rows(3, m),
            *(rows(m) for _ in range(3)),
            *(rows(3, m) for _ in range(2)),
            rows(m),
            *(rows(n) for _ in range(2)),
            *(rows(m) for _ in range(2)),
            rows(2, n),
            *(rows(3, n) for _ in range(2)),
            rows(3, m),
            *(rows(7, n) for _ in range(2)),
        ],
        name="solve",
    )(whole, place, protein_vel)
    return (protein_velocity, water_velocity)


def solution(mesh):
    in_specs = (
        P(None, ("rep", "dom")),
        P(None, ("rep", "dom")),
        P(("rep", "dom")),
        P(None, ("rep", "dom")),
        P(("rep", "dom")),
        P(("rep", "dom")),
        P(None, ("rep", "dom")),
        P(None, ("rep", "dom")),
    )
    out_specs = (P(None, ("rep", "dom")), P(None, ("rep", "dom")))
    return jax.shard_map(
        on_device, mesh=mesh, in_specs=in_specs, out_specs=out_specs, check_vma=False
    )
```

time: 801 us -> 80.5 us (0.10)
  the two profiles are of different devices: /device:TPU:1 before, /device:TPU:2 now
where the time goes in v2:
time: 80.5 us; the launch traced here: 80.3 us
  waiting for transfers between devices  40.4 us (50%)
  Pallas kernels  25.9 us (32%)
  between operations  14 us (17%)
    all_gather x1, waiting for transfers between devices, on_device(): whole = lax.all_gather(pay, 'dom', axis=0, tiled=True)  40.4 us
    pallas_call x1, Pallas kernels, on_device(): pl.pallas_call(solve, out_shape=jax.ShapeDtypeStruct(protein_vel.shape, f...  20.4 us
    pallas_call x1, Pallas kernels, on_device(): pl.pallas_call(prepare, out_shape=(jax.ShapeDtypeStruct((ROWS, LANES), f3...  5.45 us
  transfers between devices with their start and end apart: 1, of which 1 were waited for; matrix products, arithmetic and copies ran while one was open for 0% of the time, Pallas kernels for 0%

profile of v2, /device:TPU:2, one launch (start us, length us, event | category | flops | bytes accessed | tf_op | source)
XLA Modules:
  0.0 80.3 jit_solution(263722910353101321)
XLA Ops:
  7.2 0.0 all-gather.2.cloned.1.call-start
  7.2 5.4 %prepare.1 = (f32[272,128]{1,0:T(8,128)}, s32[16,128]{1,0:T(8,128)}, f32[9,1024]{1,0:T(8,128)}) custom-call(f32[3,2048]{1,0:T(4,128)} %pos.1, f32[3,2048]{1,0:T(4,128)} %vel.3, f32[16,128]{1,0:T(8,128)} %bitcast.3, s32[2,1280]{1,0:T(2,128)} %bonds.1, s32[3,128]{1,0:T(4,128)} %bitcast.4, s32[3,128]{1,0:T(4,128)} %bitcast.5, f32[9,1024]{1,0:T(8,128)} %water_pos.1, ...), custom_call_target="tpu_custom_call" | custom-call | tf_op jit(solution)/shard_map/prepare/pallas_call | solution.py:611
  12.7 0.0 all-gather.2.cloned.1.call-update
  12.7 40.4 %all-gather.2.cloned.1.call-done.whole = f32[2176,128]{1,0:T(8,128)} async-done(((f32[272,128]{1,0:T(8,128)}), f32[2176,128]{1,0:T(8,128)}) %all-gather.2.cloned.1.call-update) | async-done | bytes 1114128 | tf_op jit(solution)/shard_map/all_gather | solution.py:635
  53.0 20.4 %solve.1 = f32[3,2048]{1,0:T(4,128)} custom-call(f32[2176,128]{1,0:T(8,128)} %all-gather.2.cloned.1.call-done.whole, s32[16,128]{1,0:T(8,128)} %get-tuple-element.6.place, f32[3,2048]{1,0:T(4,128)} %vel.3), custom_call_target="tpu_custom_call" | custom-call | tf_op jit(solution)/shard_map/solve/pallas_call | solution.py:641
Async XLA Ops:
  7.2 45.9 %all-gather.2.cloned.1.call-start = ((), (), s32[]{:S(2)}) async-start(), calls=%async_computation | async-start | bytes 1253376 | tf_op jit(solution)/shard_map/all_gather | solution.py:635
Sparse Core Ops, SparseCore 0:
  12.8 40.1 all-gather.1

commit v3 on v2

--- a/solution.py
+++ b/solution.py
@@ -28,14 +28,15 @@
 BOND_ROWS = 10
 SLOT_ROWS = 3
 END_ROWS = 2 * BOND_ROWS
+HALF = BOND_ROWS * LANES
 CROSS_ROWS = 2 * SLOT_ROWS
-HALF = BOND_ROWS * LANES
 NEAR = 3
 NONE = 4095
+UNROLLED = True
 
 DIFF, VELO, SCAL = 0, 3 * END_ROWS, 6 * END_ROWS
-MASS, ATOM, MATE, LINK = (k * END_ROWS for k in (7, 8, 9, 10))
-CPOS = 11 * END_ROWS
+MASS, MATE, NAME = (k * END_ROWS for k in (7, 8, 9))
+CPOS = 10 * END_ROWS
 CVEL, CMAS, HOST = CPOS + 3 * CROSS_ROWS, CPOS + 6 * CROSS_ROWS, CPOS + 7 * CROSS_ROWS
 ROWS = -(-(CPOS + 8 * CROSS_ROWS) // 8) * 8
 
@@ -148,40 +149,61 @@
     bits = reg_bits + 10
     base = (lane * 8 + sub) << reg_bits
 
+    def ordered(bit, size, here, there):
+        turned = base >> bit if size == bits else (base >> bit) ^ (base >> size)
+        return jnp.where((turned & 1) == 0, jnp.minimum(here, there), jnp.maximum(here, there))
+
+    def registers(keys, bit, size):
+        out = list(keys)
+        for reg in range(len(keys)):
+            if reg & (1 << bit):
+                continue
+            other = reg | (1 << bit)
+            low = jnp.minimum(keys[reg], keys[other])
+            high = jnp.maximum(keys[reg], keys[other])
+            if size == bits:
+                out[reg], out[other] = low, high
+            elif size < reg_bits:
+                out[reg], out[other] = (high, low) if reg & (1 << size) else (low, high)
+            else:
+                rising = ((base >> size) & 1) == 0
+                out[reg] = jnp.where(rising, low, high)
+                out[other] = jnp.where(rising, high, low)
+        return out
+
+    def sublanes(key, bit, size):
+        step = 1 << (bit - reg_bits)
+        if step == 4:
+            mate = pltpu.roll(key, 4, 0)
+        else:
+            mate = jnp.where((sub & step) != 0, pltpu.roll(key, step, 0), pltpu.roll(key, 8 - step, 0))
+        return ordered(bit, size, key, mate)
+
+    def lanes(key, group, size):
+        steps = [1 << (bit - reg_bits - 3) for bit in group]
+        reach = [0]
+        for step in steps:
+            reach = reach + [far ^ step for far in reach]
+        values = {far: lanes_of(key, lane ^ far) if far else key for far in reach}
+        for bit, step in zip(group, steps):
+            values = {
+                far: ordered(bit, size, values[far], values[far ^ step])
+                for far in values
+                if far < step
+            }
+        return values[0]
+
     for size in range(1, bits + 1):
-        for bit in range(size - 1, -1, -1):
+        crossing = [bit for bit in range(size - 1, reg_bits + 2, -1)]
+        while crossing:
+            width = {4: 2, 2: 2, 1: 1}.get(len(crossing), 3)
+            group, crossing = crossing[:width], crossing[width:]
+            keys = [lanes(key, group, size) for key in keys]
+        for bit in range(min(size - 1, reg_bits + 2), -1, -1):
             if bit < reg_bits:
-                out = list(keys)
-                for reg in range(len(keys)):
-                    if reg & (1 << bit):
-                        continue
-                    other = reg | (1 << bit)
-                    low = jnp.minimum(keys[reg], keys[other])
-                    high = jnp.maximum(keys[reg], keys[other])
-                    if size == bits:
-                        out[reg], out[other] = low, high
-                    elif size < reg_bits:
-                        out[reg], out[other] = (high, low) if reg & (1 << size) else (low, high)
-                    else:
-                        rising = ((base >> size) & 1) == 0
-                        out[reg] = jnp.where(rising, low, high)
-                        out[other] = jnp.where(rising, high, low)
-                keys = out
-                continue
-            turned = base >> bit if size == bits else (base >> bit) ^ (base >> size)
-            keep = (turned & 1) == 0
-            out = []
-            for key in keys:
-                step = 1 << (bit - reg_bits)
-                if step == 4:
-                    mate = pltpu.roll(key, 4, 0)
-                elif step < 4:
-                    upper = (sub & step) != 0
-                    mate = jnp.where(upper, pltpu.roll(key, step, 0), pltpu.roll(key, 8 - step, 0))
-                else:
-                    mate = lanes_of(key, lane ^ (step // 8))
-                out.append(jnp.where(keep, jnp.minimum(key, mate), jnp.maximum(key, mate)))
-            keys = out
+                keys = registers(keys, bit, size)
+            else:
+                keys = [sublanes(key, bit, size) for key in keys]
     return keys
 
 
@@ -209,11 +231,23 @@
 
 
 def prepare(
-    pos, vel, mass, bonds, left, right, water_pos, water_vel, pay, place, water_out, atoms, ranked, slots, wet
+    bonds_in, right_in, left_in, pos_in, vel_in, mass_in, water_pos_in, water_vel_in, pay, place, water_out,
+    bonds, right, left, pos, vel, mass, water_pos, water_vel, atoms, ranked, slots, wet, arrived,
 ):
     lane = lax.broadcasted_iota(jnp.int32, (8, LANES), 1)
     sub = lax.broadcasted_iota(jnp.int32, (8, LANES), 0)
     f32, i32 = jnp.float32, jnp.int32
+
+    sources = (bonds_in, right_in, left_in, pos_in, vel_in, mass_in, water_pos_in, water_vel_in)
+    targets = (bonds, right, left, pos, vel, mass, water_pos, water_vel)
+    copies = [
+        pltpu.make_async_copy(source, target, arrived.at[k])
+        for k, (source, target) in enumerate(zip(sources, targets))
+    ]
+    for copy in copies:
+        copy.start()
+    for copy in copies:
+        copy.wait()
 
     def index(k):
         return (k * 8 + sub) * LANES + lane
@@ -231,15 +265,18 @@
     keys = [(atoms[8 * k : 8 * k + 8, :] * 4096 + index(k)).astype(f32) for k in range(4)]
     keys = sort_keys(keys)
     for k in range(4):
-        ranked[8 * k : 8 * k + 8, :] = keys[k]
+        ranked[pl.ds(k, 8, stride=4), :] = keys[k]
     slots[...] = sort_keys([(crossed * 1024 + index(0)).astype(f32)])[0]
 
     own, far, mates = [], [], []
+    quads = []
+    for j in range(8):
+        quad = ranked[4 * j : 4 * j + 4, :]
+        quads.append(jnp.concatenate([quad, quad], axis=0))
     for k in range(3):
         rank = lane * END_ROWS + k * 8 + sub
-        key = gather_rows(
-            functools.partial(spread, ranked), 32, (rank & 3) * 8 + ((rank >> 2) & 7), rank >> 5
-        ).astype(i32)
+        masks = bits_of((rank >> 2) & 7, 8)
+        key = pick(lambda j: lanes_of(quads[j], rank >> 5), 8, masks).astype(i32)
         end = key & 4095
         mate = jnp.where(end < HALF, end + HALF, end - HALF)
         other = gather_rows(functools.partial(spread, atoms), END_ROWS, mate >> 7, mate & 127)
@@ -260,10 +297,9 @@
         slots, 8, [((a + 1) * 1024).astype(f32) for a in own] + [((index(k) + 1) * 1024).astype(f32) for k in range(2)]
     )
     for k in range(3):
-        put(ATOM, k, own[k])
         put(MATE, k, inside[k][0])
         best = outside[k][1]
-        put(LINK, k, jnp.where(best >> 10 == own[k], best & 1023, NONE))
+        put(NAME, k, jnp.where(best >> 10 == own[k], best & 1023, own[k] + 1024))
     rank, best = inside[3]
     host = jnp.where(best >> 12 == crossed, rank - 1, NONE)
     pay[HOST : HOST + CROSS_ROWS, :] = host[:CROSS_ROWS].astype(f32)
@@ -314,8 +350,8 @@
 
 def solve(
     whole, place, vel, out,
-    mate_row, mate_col, link_row, link_col, host_row, host_col, atom, mass, push, length, scale, diff, drift,
-    below, above, near, hinge, edge, edge_mass, edge_length, edge_scale, edge_diff, edge_drift, anchor,
+    mate_row, mate_col, link_row, link_col, host_row, host_col, name, mass, push, length, scale, diff, drift,
+    below, above, near, hinge, hinges, edge, edge_mass, edge_length, edge_scale, edge_diff, edge_drift, anchor,
     now, total, now_edge, total_edge, part, ties, moved, moved_edge, run, more,
 ):
     zero = jnp.zeros((8, LANES), jnp.float32)
@@ -346,10 +382,10 @@
     for v in ends:
         row, col = place_of(load(MATE + v).astype(jnp.int32))
         mate_row[v], mate_col[v] = row, col
-        slot = load(LINK + v).astype(jnp.int32)
+        mass[v] = load(MASS + v)
+        name[v] = load(NAME + v)
+        slot = name[v].astype(jnp.int32)
         link_row[v], link_col[v] = slot >> 7, slot & 127
-        mass[v] = load(MASS + v)
-        atom[v] = load(ATOM + v)
     for r in range(CROSS_ROWS):
         row, col = place_of(load(HOST + r).astype(jnp.int32))
         host_row[r], host_col[r] = row, jnp.minimum(col, LANES - 1)
@@ -386,7 +422,7 @@
     for r, x in enumerate(both(start)):
         now_edge[r], total_edge[r] = x, x
 
-    names = around([atom[v] for v in ends])
+    names = around([name[v] for v in ends])
     many = jnp.zeros((8, LANES), jnp.int32)
     fields = [around([push[c, v] for v in ends]) for c in every]
     for v in ends:
@@ -398,7 +434,7 @@
             above[s - 1, v] = jnp.where(
                 names[v] == names[v + s], dot3(here, [fields[c][v + s] for c in every]), 0.0
             )
-        past = names[v - 4] if v >= 1 else pltpu.roll(atom[END_ROWS - 4], 1, 1)
+        past = names[v - 4] if v >= 1 else pltpu.roll(name[END_ROWS - 4], 1, 1)
         many = jnp.where(names[v] == past, 1, many)
         masks = bits_of(link_row[v], CROSS_ROWS)
         linked = link_row[v] < CROSS_ROWS
@@ -407,6 +443,10 @@
             ties[c, v] = jnp.where(linked, mass[v] * across[c], 0.0)
         hinge[v] = jnp.where(linked, dot3(here, across), 0.0)
     crowded = jnp.max(many) > 0
+    bound = around([hinge[v] for v in ends])
+    for v in ends:
+        for s in range(1, NEAR + 1):
+            hinges[s - 1, v] = jnp.where(near[s - 1, v] > 0.5, bound[v - s], 0.0)
 
     def gated(factor, value):
         return jnp.where(factor != 0.0, factor * value, 0.0)
@@ -422,7 +462,7 @@
                 wrap = jnp.where(source < 0, 1, 0) if forward else jnp.where(source >= END_ROWS, 1, 0)
                 source = source + wrap * END_ROWS if forward else source - wrap * END_ROWS
                 shift = turns + wrap if forward else (LANES - turns - wrap)
-                match = atom[v] == pltpu.roll(atom[source], shift, 1)
+                match = name[v] == pltpu.roll(name[source], shift, 1)
                 for r in rows:
                     more[r, v] = run[r, v] + jnp.where(match, pltpu.roll(run[r, source], shift, 1), 0.0)
                 return carry
@@ -458,21 +498,10 @@
             got.append(value)
         return got
 
-    def apply(order, carry):
+    def apply(slow):
         x = around([now[v] for v in ends])
-        bound = {v: gated(hinge[v], x[v]) for v in ends}
-        wide = around([bound[v] for v in ends])
-        for v in ends:
-            sum_x, sum_bound = zero, bound[v]
-            for s in range(1, NEAR + 1):
-                sum_x = sum_x + gated(below[s - 1, v], x[v - s])
-                sum_x = sum_x + gated(above[s - 1, v], x[v + s])
-                sum_bound = sum_bound + jnp.where(near[s - 1, v] > 0.5, wide[v - s], 0.0)
-            part[0, v] = sum_x
-            part[1, v] = sum_bound
-
-        @pl.when(crowded)
-        def _():
+        crossing = [now_edge[r] for r in range(CROSS_ROWS)]
+        if slow:
             scan_fields(now)
 
             def fill(v, carry):
@@ -483,23 +512,29 @@
                 return carry
 
             lax.fori_loop(0, END_ROWS, fill, 0)
-
-        crossing = [now_edge[r] for r in range(CROSS_ROWS)]
-        whole_part = []
+        sums, bounds = [], []
         for v in ends:
+            if slow:
+                sum_x, sum_bound = part[0, v], part[1, v]
+            else:
+                sum_x, sum_bound = zero, gated(hinge[v], x[v])
+                for s in range(1, NEAR + 1):
+                    sum_x = sum_x + gated(below[s - 1, v], x[v - s])
+                    sum_x = sum_x + gated(above[s - 1, v], x[v + s])
+                    sum_bound = sum_bound + gated(hinges[s - 1, v], x[v - s])
             value = choose(crossing, CROSS_ROWS, bits_of(link_row[v], CROSS_ROWS), link_col[v])
-            whole_part.append(part[0, v] + gated(hinge[v], value))
-        pulled = at_edges([part[1, v] for v in ends])
+            sums.append(sum_x + gated(hinge[v], value))
+            bounds.append(sum_bound)
+        pulled = at_edges(bounds)
         pulled = [jnp.where(anchor[r] > 0.5, pulled[r], 0.0) for r in range(CROSS_ROWS)]
         for r, value in enumerate(both([-(pulled[r] + up(pulled[r + SLOT_ROWS])) for r in right])):
             now_edge[r] = value
             total_edge[r] = total_edge[r] + value
         for v in ends:
-            value = choose(whole_part, END_ROWS, bits_of(mate_row[v], END_ROWS), mate_col[v])
-            value = -(whole_part[v] + value)
+            value = choose(sums, END_ROWS, bits_of(mate_row[v], END_ROWS), mate_col[v])
+            value = -(sums[v] + value)
             now[v] = value
             total[v] = total[v] + value
-        return carry
 
     def edges_moved():
         got = []
@@ -514,21 +549,15 @@
             )
         return got
 
-    def turn(index, carry):
-        lax.fori_loop(0, ORDER, apply, 0)
-
-        x = [total[v] for v in ends]
-        for c in every:
-            field = around([push[c, v] * x[v] for v in ends])
-            for v in ends:
-                value = field[v]
-                for s in range(1, NEAR + 1):
-                    value = value + jnp.where(names_equal(v, -s), field[v - s], 0.0)
-                    value = value + jnp.where(names_equal(v, s), field[v + s], 0.0)
-                run[c, v] = value
-
-        @pl.when(crowded)
-        def _():
+    def same(v, s):
+        if s < 0:
+            return near[-s - 1, v] > 0.5
+        if v + s < END_ROWS:
+            return near[s - 1, v + s] > 0.5
+        return pltpu.roll(near[s - 1, v + s - END_ROWS], LANES - 1, 1) > 0.5
+
+    def move(slow):
+        if slow:
             scan_fields(total)
 
             def fill(v, carry):
@@ -537,7 +566,16 @@
                 return carry
 
             lax.fori_loop(0, END_ROWS, fill, 0)
-
+        else:
+            x = [total[v] for v in ends]
+            for c in every:
+                field = around([push[c, v] * x[v] for v in ends])
+                for v in ends:
+                    value = field[v]
+                    for s in range(1, NEAR + 1):
+                        value = value + jnp.where(same(v, -s), field[v - s], 0.0)
+                        value = value + jnp.where(same(v, s), field[v + s], 0.0)
+                    run[c, v] = value
         crossing = [total_edge[r] for r in range(CROSS_ROWS)]
         for v in ends:
             value = choose(crossing, CROSS_ROWS, bits_of(link_row[v], CROSS_ROWS), link_col[v])
@@ -548,43 +586,55 @@
             for c in every:
                 moved_edge[c, r] = moved_edge[c, r] + edge_mass[r] * edge[c, r] * crossing[r]
 
-        def correct(d, g, size, s):
+    def correct():
+        def rate(d, g, size, s):
             excess = 2.0 * dot3(d, g) + dot3(g, g)
             return s * excess / (size + jnp.sqrt(size * size - excess))
 
-        @pl.when(index < ITER)
-        def _():
-            here = edges_moved()
-            start = []
-            for r in right:
-                g = [edge_drift[c, r] - (here[r][c] - up(here[r + SLOT_ROWS][c])) for c in every]
-                start.append(correct([edge_diff[c, r] for c in every], g, edge_length[r], edge_scale[r]))
-            for r, value in enumerate(both(start)):
-                now_edge[r], total_edge[r] = value, value
-            for v in ends:
-                masks = bits_of(mate_row[v], END_ROWS)
-                there = [choose([moved[c, w] for w in ends], END_ROWS, masks, mate_col[v]) for c in every]
-                g = [drift[c, v] - (moved[c, v] - there[c]) for c in every]
-                value = correct([diff[c, v] for c in every], g, length[v], scale[v])
-                now[v], total[v] = value, value
-
-        return carry
-
-    def names_equal(v, s):
-        flag = near[s - 1, v + s] if s > 0 and v + s < END_ROWS else None
-        if s < 0:
-            flag = near[-s - 1, v]
-        elif flag is None:
-            flag = pltpu.roll(near[s - 1, v + s - END_ROWS], LANES - 1, 1)
-        return flag > 0.5
-
-    lax.fori_loop(0, ITER + 1, turn, 0)
+        here = edges_moved()
+        start = []
+        for r in right:
+            g = [edge_drift[c, r] - (here[r][c] - up(here[r + SLOT_ROWS][c])) for c in every]
+            start.append(rate([edge_diff[c, r] for c in every], g, edge_length[r], edge_scale[r]))
+        for r, value in enumerate(both(start)):
+            now_edge[r], total_edge[r] = value, value
+        for v in ends:
+            masks = bits_of(mate_row[v], END_ROWS)
+            there = [choose([moved[c, w] for w in ends], END_ROWS, masks, mate_col[v]) for c in every]
+            g = [drift[c, v] - (moved[c, v] - there[c]) for c in every]
+            value = rate([diff[c, v] for c in every], g, length[v], scale[v])
+            now[v], total[v] = value, value
+
+    def rounds(slow):
+        def one(order, carry):
+            apply(slow)
+            return carry
+
+        def turn(index, carry):
+            if slow or not UNROLLED:
+                lax.fori_loop(0, ORDER, one, 0)
+            else:
+                for order in range(ORDER):
+                    apply(slow)
+            move(slow)
+
+            @pl.when(index < ITER)
+            def _():
+                correct()
+
+            return carry
+
+        lax.fori_loop(0, ITER + 1, turn, 0)
+
+    @pl.when(crowded)
+    def _():
+        rounds(True)
+
+    @pl.when(jnp.logical_not(crowded))
+    def _():
+        rounds(False)
 
     me = lax.axis_index("dom")
-    edges = edges_moved()
-    for r in range(CROSS_ROWS):
-        for c in every:
-            moved_edge[c, r] = edges[r][c]
     own = [
         [jnp.broadcast_to(moved[c, v, pl.ds(me, 1), :], (8, LANES)) for v in ends]
         + [jnp.broadcast_to(moved_edge[c, r, pl.ds(me, 1), :], (8, LANES)) for r in range(CROSS_ROWS)]
@@ -607,31 +657,36 @@
     protein_pos, protein_vel, inv_mass, bond_atoms, left_atoms, right_atoms, water_pos, water_vel
 ):
     f32, i32 = jnp.float32, jnp.int32
-    mass = inv_mass.reshape(ATOM_ROWS, LANES)
+    inputs = (
+        bond_atoms,
+        right_atoms.reshape(SLOT_ROWS, LANES),
+        left_atoms.reshape(SLOT_ROWS, LANES),
+        protein_pos,
+        protein_vel,
+        inv_mass.reshape(ATOM_ROWS, LANES),
+        water_pos,
+        water_vel,
+    )
+    inputs = [pltpu.with_memory_space_constraint(x, pltpu.HBM) for x in inputs]
     pay, place, water_velocity = pl.pallas_call(
         prepare,
+        in_specs=[pl.BlockSpec(memory_space=pltpu.HBM)] * len(inputs),
         out_shape=(
             jax.ShapeDtypeStruct((ROWS, LANES), f32),
             jax.ShapeDtypeStruct((ATOM_ROWS, LANES), i32),
             jax.ShapeDtypeStruct(water_pos.shape, f32),
         ),
         scratch_shapes=[
+            *(pltpu.VMEM(x.shape, x.dtype) for x in inputs),
             pltpu.VMEM((40, LANES), i32),
             pltpu.VMEM((32, LANES), f32),
             pltpu.VMEM((8, LANES), f32),
             pltpu.VMEM((18, 8, LANES), f32),
+            pltpu.SemaphoreType.DMA((len(inputs),)),
         ],
+        compiler_params=pltpu.CompilerParams(vmem_limit_bytes=8 << 20),
         name="prepare",
-    )(
-        protein_pos,
-        protein_vel,
-        mass,
-        bond_atoms,
-        left_atoms.reshape(SLOT_ROWS, LANES),
-        right_atoms.reshape(SLOT_ROWS, LANES),
-        water_pos,
-        water_vel,
-    )
+    )(*inputs)
     whole = lax.all_gather(pay, "dom", axis=0, tiled=True)
 
     def rows(*lead, dtype=f32):
@@ -650,6 +705,7 @@
             *(rows(3, n) for _ in range(2)),
             *(rows(NEAR, n) for _ in range(3)),
             rows(n),
+            rows(NEAR, n),
             rows(3, m),
             *(rows(m) for _ in range(3)),
             *(rows(3, m) for _ in range(2)),
@@ -661,6 +717,7 @@
             rows(3, m),
             *(rows(7, n) for _ in range(2)),
         ],
+        compiler_params=pltpu.CompilerParams(vmem_limit_bytes=16 << 20),
         name="solve",
     )(whole, place, protein_vel)
     return (protein_velocity, water_velocity)

time: 80.5 us -> 41 us (0.51)
  the two profiles are of different devices: /device:TPU:2 before, /device:TPU:1 now
where the time goes in v3:
time: 41 us; the launch traced here: 40.8 us
  Pallas kernels  21.1 us (51%)
  blocking collectives  19 us (46%)
  between operations  0.65 us (2%)
    all_gather x1, blocking collectives, on_device(): whole = lax.all_gather(pay, 'dom', axis=0, tiled=True)  19 us
    pallas_call x1, Pallas kernels, on_device(): pl.pallas_call(solve, out_shape=jax.ShapeDtypeStruct(protein_vel.shape, f...  16.3 us
    pallas_call x1, Pallas kernels, on_device(): pl.pallas_call(prepare, in_specs=[pl.BlockSpec(memory_space=pltpu.HBM)] *...  4.81 us

profile of v3, /device:TPU:1, one launch (start us, length us, event | category | flops | bytes accessed | tf_op | source)
XLA Modules:
  0.0 40.8 jit_solution(5019412366374734070)
XLA Ops:
  0.6 4.8 %prepare.1 = (f32[248,128]{1,0:T(8,128)S(1)}, s32[16,128]{1,0:T(8,128)S(1)}, f32[9,1024]{1,0:T(8,128)}) custom-call(s32[2,1280]{1,0:T(2,128)} %bonds_in.1, s32[3,128]{1,0:T(4,128)} %bitcast.4, s32[3,128]{1,0:T(4,128)} %bitcast.5, f32[3,2048]{1,0:T(4,128)} %pos_in.1, f32[3,2048]{1,0:T(4,128)} %vel.1, f32[16,128]{1,0:T(8,128)} %bitcast.3, ...), custom_call_target="tpu_custom_call" | custom-call | tf_op jit(solution)/shard_map/prepare/pallas_call | solution.py:671
  5.5 0.0 copy-start
  5.5 19.0 %all_gather.3.whole = f32[1984,128]{1,0:T(8,128)S(1)} all-gather(f32[248,128]{1,0:T(8,128)S(1)} %get-tuple-element.5), channel_id=1, replica_groups=mesh['rep'=32,'dom'=8] {'dom'}, dimensions={0}, use_global_device_ids=true | all-gather | bytes 1142784 | tf_op jit(solution)/shard_map/all_gather | solution.py:690
  24.5 0.0 copy-done
  24.5 16.3 %solve.1 = f32[3,2048]{1,0:T(4,128)} custom-call(f32[1984,128]{1,0:T(8,128)S(1)} %all_gather.3.whole, s32[16,128]{1,0:T(8,128)S(1)} %get-tuple-element.6.place, f32[3,2048]{1,0:T(4,128)S(1)} %copy-done), custom_call_target="tpu_custom_call" | custom-call | tf_op jit(solution)/shard_map/solve/pallas_call | solution.py:696
Async XLA Ops:
  5.5 19.0 %copy-start = (f32[3,2048]{1,0:T(4,128)S(1)}, f32[3,2048]{1,0:T(4,128)}, u32[]{:S(2)}) copy-start(f32[3,2048]{1,0:T(4,128)} %vel.1) | copy-start | bytes 73732

commit v4 on v3

--- a/solution.py
+++ b/solution.py
@@ -32,7 +32,6 @@
 CROSS_ROWS = 2 * SLOT_ROWS
 NEAR = 3
 NONE = 4095
-UNROLLED = True
 
 DIFF, VELO, SCAL = 0, 3 * END_ROWS, 6 * END_ROWS
 MASS, MATE, NAME = (k * END_ROWS for k in (7, 8, 9))
@@ -231,15 +230,15 @@
 
 
 def prepare(
-    bonds_in, right_in, left_in, pos_in, vel_in, mass_in, water_pos_in, water_vel_in, pay, place, water_out,
-    bonds, right, left, pos, vel, mass, water_pos, water_vel, atoms, ranked, slots, wet, arrived,
+    bonds_in, right_in, left_in, pos_in, vel_in, mass_in, pay, place,
+    bonds, right, left, pos, vel, mass, atoms, ranked, slots, arrived,
 ):
     lane = lax.broadcasted_iota(jnp.int32, (8, LANES), 1)
     sub = lax.broadcasted_iota(jnp.int32, (8, LANES), 0)
     f32, i32 = jnp.float32, jnp.int32
 
-    sources = (bonds_in, right_in, left_in, pos_in, vel_in, mass_in, water_pos_in, water_vel_in)
-    targets = (bonds, right, left, pos, vel, mass, water_pos, water_vel)
+    sources = (bonds_in, right_in, left_in, pos_in, vel_in, mass_in)
+    targets = (bonds, right, left, pos, vel, mass)
     copies = [
         pltpu.make_async_copy(source, target, arrived.at[k])
         for k, (source, target) in enumerate(zip(sources, targets))
@@ -333,26 +332,13 @@
         put(SCAL, k, 1.0 / jnp.sqrt(values[k] + values[3 + k]))
     pay[CMAS : CMAS + CROSS_ROWS, :] = values[6][:CROSS_ROWS]
 
-    for j in range(8):
-        cut = slice(j * LANES, (j + 1) * LANES)
-        for c in range(9):
-            wet[c, j : j + 1, :] = water_pos[c : c + 1, cut]
-            wet[9 + c, j : j + 1, :] = water_vel[c : c + 1, cut]
-    before = [wet[c] for c in range(9)]
-    speed = [wet[9 + c] for c in range(9)]
-    after = [before[c] + time_step * speed[c] for c in range(9)]
-    settled = settle(before, after)
-    for c in range(9):
-        result = speed[c] + (settled[c] - after[c]) / time_step
-        for j in range(8):
-            water_out[c : c + 1, j * LANES : (j + 1) * LANES] = result[j : j + 1, :]
-
 
 def solve(
-    whole, place, vel, out,
+    whole, place, vel, water_pos, water_vel, out, water_home,
     mate_row, mate_col, link_row, link_col, host_row, host_col, name, mass, push, length, scale, diff, drift,
     below, above, near, hinge, hinges, edge, edge_mass, edge_length, edge_scale, edge_diff, edge_drift, anchor,
-    now, total, now_edge, total_edge, part, ties, moved, moved_edge, run, more,
+    now, total, now_edge, total_edge, part, ties, moved, moved_edge, run, more, mine, index, shown,
+    wet, water_out, leaving,
 ):
     zero = jnp.zeros((8, LANES), jnp.float32)
     every, ends, right = range(3), range(END_ROWS), range(SLOT_ROWS)
@@ -378,6 +364,22 @@
 
     def both(values):
         return values + [down(x) for x in values]
+
+    for j in range(8):
+        cut = slice(j * LANES, (j + 1) * LANES)
+        for c in range(9):
+            wet[c, j : j + 1, :] = water_pos[c : c + 1, cut]
+            wet[9 + c, j : j + 1, :] = water_vel[c : c + 1, cut]
+    here = [wet[c] for c in range(9)]
+    speed = [wet[9 + c] for c in range(9)]
+    there = [here[c] + time_step * speed[c] for c in range(9)]
+    settled = settle(here, there)
+    for c in range(9):
+        result = speed[c] + (settled[c] - there[c]) / time_step
+        for j in range(8):
+            water_out[c : c + 1, j * LANES : (j + 1) * LANES] = result[j : j + 1, :]
+    drained = pltpu.make_async_copy(water_out, water_home, leaving)
+    drained.start()
 
     for v in ends:
         row, col = place_of(load(MATE + v).astype(jnp.int32))
@@ -498,7 +500,7 @@
             got.append(value)
         return got
 
-    def apply(slow):
+    def apply(slow, last=False):
         x = around([now[v] for v in ends])
         crossing = [now_edge[r] for r in range(CROSS_ROWS)]
         if slow:
@@ -530,6 +532,10 @@
         for r, value in enumerate(both([-(pulled[r] + up(pulled[r + SLOT_ROWS])) for r in right])):
             now_edge[r] = value
             total_edge[r] = total_edge[r] + value
+        if last:
+            for v in ends:
+                part[0, v] = sums[v]
+            return
         for v in ends:
             value = choose(sums, END_ROWS, bits_of(mate_row[v], END_ROWS), mate_col[v])
             value = -(sums[v] + value)
@@ -582,9 +588,7 @@
             linked = link_row[v] < CROSS_ROWS
             for c in every:
                 moved[c, v] = moved[c, v] + mass[v] * run[c, v] + jnp.where(linked, ties[c, v] * value, 0.0)
-        for r in range(CROSS_ROWS):
-            for c in every:
-                moved_edge[c, r] = moved_edge[c, r] + edge_mass[r] * edge[c, r] * crossing[r]
+        edge_sums()
 
     def correct():
         def rate(d, g, size, s):
@@ -605,26 +609,108 @@
             value = rate([diff[c, v] for c in every], g, length[v], scale[v])
             now[v], total[v] = value, value
 
+    me = lax.axis_index("dom")
+    bands = range(3)
+
+    def take(target, place, source):
+        for v in ends:
+            target[place, v : v + 1, :] = source(v)[pl.ds(me, 1), :]
+
+    def band(ref, place, k):
+        return ref[place, 8 * k : 8 * k + 8, :]
+
+    def spots(place, k):
+        return band(index, place, k) & (LANES - 1)
+
+    def show(place, values):
+        for k in bands:
+            shown[place, 4 + 8 * k : min(12 + 8 * k, 24), :] = values[k][: min(8, END_ROWS - 8 * k)]
+        shown[place, 0:4, :] = pltpu.roll(values[2], 1, 1)[0:4]
+        shown[place, 24:28, :] = pltpu.roll(values[0], LANES - 1, 1)[0:4]
+
+    def shifted(place, k, step):
+        return shown[place, 4 + 8 * k + step : 12 + 8 * k + step, :]
+
+    def edge_sums():
+        for r in range(CROSS_ROWS):
+            for c in every:
+                moved_edge[c, r] = moved_edge[c, r] + edge_mass[r] * edge[c, r] * total_edge[r]
+
+    def finish():
+        take(mine, 3, lambda v: part.at[0, v])
+        take(mine, 4, lambda v: total.at[v])
+        for c in every:
+            take(mine, c, lambda v: moved.at[c, v])
+        crossing = [jnp.broadcast_to(total_edge[r, pl.ds(me, 1), :], (8, LANES)) for r in range(CROSS_ROWS)]
+        x, links = [], []
+        for k in bands:
+            masks = bits_of(band(index, 0, k), END_ROWS)
+            value = pick(
+                lambda r: lanes_of(jnp.broadcast_to(mine[3, r : r + 1, :], (8, LANES)), spots(1, k)),
+                END_ROWS,
+                masks,
+            )
+            x.append(band(mine, 4, k) - (band(mine, 3, k) + value))
+            masks = bits_of(band(index, 2, k), CROSS_ROWS)
+            links.append(choose(crossing, CROSS_ROWS, masks, spots(3, k)))
+        show(3, [band(mine, 5, k) for k in bands])
+        for c in every:
+            show(c, [band(mine, 6 + c, k) * x[k] for k in bands])
+        for k in bands:
+            linked = band(index, 2, k) < CROSS_ROWS
+            value = [shifted(c, k, 0) for c in every]
+            for step in (-3, -2, -1, 1, 2, 3):
+                same = shifted(3, k, step) == band(mine, 5, k)
+                value = [value[c] + jnp.where(same, shifted(c, k, step), 0.0) for c in every]
+            for c in every:
+                mine[c, 8 * k : 8 * k + 8, :] = (
+                    band(mine, c, k)
+                    + band(mine, 12, k) * value[c]
+                    + jnp.where(linked, band(mine, 9 + c, k) * links[k], 0.0)
+                )
+
     def rounds(slow):
-        def one(order, carry):
-            apply(slow)
+        if slow:
+
+            def one(order, carry):
+                apply(True)
+                return carry
+
+            def turn(turns, carry):
+                lax.fori_loop(0, ORDER, one, 0)
+                move(True)
+
+                @pl.when(turns < ITER)
+                def _():
+                    correct()
+
+                return carry
+
+            lax.fori_loop(0, ITER + 1, turn, 0)
+            for c in every:
+                take(mine, c, lambda v: moved.at[c, v])
+            return
+
+        take(mine, 5, lambda v: name.at[v])
+        take(mine, 12, lambda v: mass.at[v])
+        for c in every:
+            take(mine, 6 + c, lambda v: push.at[c, v])
+            take(mine, 9 + c, lambda v: ties.at[c, v])
+        for place_in, source in enumerate((mate_row, mate_col, link_row, link_col)):
+            take(index, place_in, lambda v: source.at[v])
+
+        def turn(turns, carry):
+            for order in range(ORDER):
+                apply(False)
+            move(False)
+            correct()
             return carry
 
-        def turn(index, carry):
-            if slow or not UNROLLED:
-                lax.fori_loop(0, ORDER, one, 0)
-            else:
-                for order in range(ORDER):
-                    apply(slow)
-            move(slow)
-
-            @pl.when(index < ITER)
-            def _():
-                correct()
-
-            return carry
-
-        lax.fori_loop(0, ITER + 1, turn, 0)
+        lax.fori_loop(0, ITER, turn, 0)
+        for order in range(ORDER):
+            apply(False, order == ORDER - 1)
+        edge_sums()
+        finish()
 
     @pl.when(crowded)
     def _():
@@ -634,9 +720,8 @@
     def _():
         rounds(False)
 
-    me = lax.axis_index("dom")
     own = [
-        [jnp.broadcast_to(moved[c, v, pl.ds(me, 1), :], (8, LANES)) for v in ends]
+        [jnp.broadcast_to(mine[c, v : v + 1, :], (8, LANES)) for v in ends]
         + [jnp.broadcast_to(moved_edge[c, r, pl.ds(me, 1), :], (8, LANES)) for r in range(CROSS_ROWS)]
         for c in every
     ]
@@ -651,6 +736,7 @@
             for j in range(8):
                 cut = slice((8 * k + j) * LANES, (8 * k + j + 1) * LANES)
                 out[c : c + 1, cut] = vel[c : c + 1, cut] - shift[j : j + 1, :]
+    drained.wait()
 
 
 def on_device(
@@ -664,24 +750,20 @@
         protein_pos,
         protein_vel,
         inv_mass.reshape(ATOM_ROWS, LANES),
-        water_pos,
-        water_vel,
     )
     inputs = [pltpu.with_memory_space_constraint(x, pltpu.HBM) for x in inputs]
-    pay, place, water_velocity = pl.pallas_call(
+    pay, place = pl.pallas_call(
         prepare,
         in_specs=[pl.BlockSpec(memory_space=pltpu.HBM)] * len(inputs),
         out_shape=(
             jax.ShapeDtypeStruct((ROWS, LANES), f32),
             jax.ShapeDtypeStruct((ATOM_ROWS, LANES), i32),
-            jax.ShapeDtypeStruct(water_pos.shape, f32),
         ),
         scratch_shapes=[
             *(pltpu.VMEM(x.shape, x.dtype) for x in inputs),
             pltpu.VMEM((40, LANES), i32),
             pltpu.VMEM((32, LANES), f32),
             pltpu.VMEM((8, LANES), f32),
-            pltpu.VMEM((18, 8, LANES), f32),
             pltpu.SemaphoreType.DMA((len(inputs),)),
         ],
         compiler_params=pltpu.CompilerParams(vmem_limit_bytes=8 << 20),
@@ -693,9 +775,13 @@
         return pltpu.VMEM((*lead, 8, LANES), dtype)
 
     n, m = END_ROWS, CROSS_ROWS
-    protein_velocity = pl.pallas_call(
+    return pl.pallas_call(
         solve,
-        out_shape=jax.ShapeDtypeStruct(protein_vel.shape, f32),
+        out_specs=(pl.BlockSpec(memory_space=pltpu.VMEM), pl.BlockSpec(memory_space=pltpu.HBM)),
+        out_shape=(
+            jax.ShapeDtypeStruct(protein_vel.shape, f32),
+            jax.ShapeDtypeStruct(water_pos.shape, f32),
+        ),
         scratch_shapes=[
             *(rows(n, dtype=i32) for _ in range(4)),
             *(rows(m, dtype=i32) for _ in range(2)),
@@ -716,11 +802,16 @@
             *(rows(3, n) for _ in range(2)),
             rows(3, m),
             *(rows(7, n) for _ in range(2)),
+            pltpu.VMEM((14, 24, LANES), f32),
+            pltpu.VMEM((4, 24, LANES), i32),
+            pltpu.VMEM((4, 32, LANES), f32),
+            pltpu.VMEM((18, 8, LANES), f32),
+            pltpu.VMEM(water_pos.shape, f32),
+            pltpu.SemaphoreType.DMA,
         ],
         compiler_params=pltpu.CompilerParams(vmem_limit_bytes=16 << 20),
         name="solve",
-    )(whole, place, protein_vel)
-    return (protein_velocity, water_velocity)
+    )(whole, place, protein_vel, water_pos, water_vel)
 
 
 def solution(mesh):

time: 41 us -> 40.2 us (0.980)
  Pallas kernels: 21.1 us -> 20.1 us
    pallas_call x1, Pallas kernels: 4.81 us -> 3.98 us  [on_device(): pl.pallas_call(prepare, in_specs=[pl.BlockSpec(memory_space=pltpu.HBM)] *...]
where the time goes in v4:
time: 40.2 us; the launch traced here: 40 us
  Pallas kernels  20.1 us (50%)
  blocking collectives  19.1 us (48%)
  between operations  0.83 us (2%)
    all_gather x1, blocking collectives, on_device(): whole = lax.all_gather(pay, 'dom', axis=0, tiled=True)  19.1 us
    pallas_call x1, Pallas kernels, on_device(): pl.pallas_call(solve, out_specs=(pl.BlockSpec(memory_space=pltpu.VMEM), p...  16.1 us
    pallas_call x1, Pallas kernels, on_device(): pl.pallas_call(prepare, in_specs=[pl.BlockSpec(memory_space=pltpu.HBM)] *...  3.98 us

profile of v4, /device:TPU:1, one launch (start us, length us, event | category | flops | bytes accessed | tf_op | source)
XLA Modules:
  0.0 40.0 jit_solution(5062254122897216490)
XLA Ops:
  0.6 4.0 %prepare.1 = (f32[248,128]{1,0:T(8,128)S(1)}, s32[16,128]{1,0:T(8,128)S(1)}) custom-call(s32[2,1280]{1,0:T(2,128)} %bonds_in.1, s32[3,128]{1,0:T(4,128)} %bitcast.4, s32[3,128]{1,0:T(4,128)} %bitcast.5, f32[3,2048]{1,0:T(4,128)} %pos_in.1, f32[3,2048]{1,0:T(4,128)} %vel.1, f32[16,128]{1,0:T(8,128)} %bitcast.3), custom_call_target="tpu_custom_call" | custom-call | tf_op jit(solution)/shard_map/prepare/pallas_call | solution.py:755
  4.6 0.0 copy-start
  4.6 0.0 copy-start.1
  4.6 0.0 copy-start.2
  4.7 19.1 %all_gather.3.whole = f32[1984,128]{1,0:T(8,128)S(1)} all-gather(f32[248,128]{1,0:T(8,128)S(1)} %get-tuple-element.4), channel_id=1, replica_groups=mesh['rep'=32,'dom'=8] {'dom'}, dimensions={0}, use_global_device_ids=true | all-gather | bytes 1142784 | tf_op jit(solution)/shard_map/all_gather | solution.py:772
  23.8 0.0 copy-done
  23.8 0.0 copy-done.1
  23.8 0.0 copy-done.2
  23.8 16.1 %solve.1 = (f32[3,2048]{1,0:T(4,128)}, f32[9,1024]{1,0:T(8,128)}) custom-call(f32[1984,128]{1,0:T(8,128)S(1)} %all_gather.3.whole, s32[16,128]{1,0:T(8,128)S(1)} %get-tuple-element.5.place, f32[3,2048]{1,0:T(4,128)S(1)} %copy-done, f32[9,1024]{1,0:T(8,128)S(1)} %copy-done.1, f32[9,1024]{1,0:T(8,128)S(1)} %copy-done.2), custom_call_target="tpu_custom_call" | custom-call | tf_op jit(solution)/shard_map/solve/pallas_call | solution.py:778
Async XLA Ops:
  4.6 19.2 %copy-start = (f32[3,2048]{1,0:T(4,128)S(1)}, f32[3,2048]{1,0:T(4,128)}, u32[]{:S(2)}) copy-start(f32[3,2048]{1,0:T(4,128)} %vel.1) | copy-start | bytes 73732
  4.6 19.1 %copy-start.1 = (f32[9,1024]{1,0:T(8,128)S(1)}, f32[9,1024]{1,0:T(8,128)}, u32[]{:S(2)}) copy-start(f32[9,1024]{1,0:T(8,128)} %water_pos.1) | copy-start | bytes 110596
  4.6 19.1 %copy-start.2 = (f32[9,1024]{1,0:T(8,128)S(1)}, f32[9,1024]{1,0:T(8,128)}, u32[]{:S(2)}) copy-start(f32[9,1024]{1,0:T(8,128)} %water_vel.1) | copy-start | bytes 110596

commit v5 on v4

--- a/solution.py
+++ b/solution.py
@@ -178,15 +178,15 @@
             mate = jnp.where((sub & step) != 0, pltpu.roll(key, step, 0), pltpu.roll(key, 8 - step, 0))
         return ordered(bit, size, key, mate)
 
-    def lanes(key, group, size):
+    def lanes(keys, group, size):
         steps = [1 << (bit - reg_bits - 3) for bit in group]
         reach = [0]
         for step in steps:
             reach = reach + [far ^ step for far in reach]
-        values = {far: lanes_of(key, lane ^ far) if far else key for far in reach}
+        values = {far: [lanes_of(key, lane ^ far) if far else key for key in keys] for far in reach}
         for bit, step in zip(group, steps):
             values = {
-                far: ordered(bit, size, values[far], values[far ^ step])
+                far: [ordered(bit, size, here, there) for here, there in zip(values[far], values[far ^ step])]
                 for far in values
                 if far < step
             }
@@ -197,7 +197,7 @@
         while crossing:
             width = {4: 2, 2: 2, 1: 1}.get(len(crossing), 3)
             group, crossing = crossing[:width], crossing[width:]
-            keys = [lanes(key, group, size) for key in keys]
+            keys = lanes(keys, group, size)
         for bit in range(min(size - 1, reg_bits + 2), -1, -1):
             if bit < reg_bits:
                 keys = registers(keys, bit, size)
@@ -210,14 +210,15 @@
     heads = table[0:1, :]
     marks = [jnp.broadcast_to(heads[:, 8 * i : 8 * i + 1], (8, LANES)) for i in range(1, 16)]
     wide = jnp.broadcast_to(heads, (8, LANES))
+    rolled = [pltpu.roll(wide, LANES - i, 1) for i in range(1, 8)]
     found = []
     for query in queries:
         group = jnp.zeros((8, LANES), jnp.int32)
         for mark in marks:
             group = group + jnp.where(mark < query, 8, 0)
         column = group
-        for i in range(1, 8):
-            column = column + jnp.where(lanes_of(wide, group + i) < query, 1, 0)
+        for turned in rolled:
+            column = column + jnp.where(lanes_of(turned, group) < query, 1, 0)
         rank = column * rows
         best = jnp.full((8, LANES), -1.0, jnp.float32)
         for r in range(rows):
@@ -231,7 +232,7 @@
 
 def prepare(
     bonds_in, right_in, left_in, pos_in, vel_in, mass_in, pay, place,
-    bonds, right, left, pos, vel, mass, atoms, ranked, slots, arrived,
+    bonds, right, left, pos, vel, mass, atoms, ranked, listed, slots, arrived,
 ):
     lane = lax.broadcasted_iota(jnp.int32, (8, LANES), 1)
     sub = lax.broadcasted_iota(jnp.int32, (8, LANES), 0)
@@ -275,7 +276,9 @@
     for k in range(3):
         rank = lane * END_ROWS + k * 8 + sub
         masks = bits_of((rank >> 2) & 7, 8)
-        key = pick(lambda j: lanes_of(quads[j], rank >> 5), 8, masks).astype(i32)
+        key = pick(lambda j: lanes_of(quads[j], rank >> 5), 8, masks)
+        listed[8 * k : 8 * k + 8, :] = key
+        key = key.astype(i32)
         end = key & 4095
         mate = jnp.where(end < HALF, end + HALF, end - HALF)
         other = gather_rows(functools.partial(spread, atoms), END_ROWS, mate >> 7, mate & 127)
@@ -288,8 +291,8 @@
         pay[block + 8 * k : block + 8 * k + count, :] = value[:count].astype(f32)
 
     inside = find(
-        ranked,
-        32,
+        listed,
+        END_ROWS,
         mates + [((crossed + 1) * 4096).astype(f32)] + [((index(k) + 1) * 4096).astype(f32) for k in range(2)],
     )
     outside = find(
@@ -315,22 +318,24 @@
     edge = jnp.minimum(crossed, 2047)
     where = [(a >> 7, a & 127) for a in own + far + [edge]]
 
-    def at_ends(table):
-        return [gather_rows(table, ATOM_ROWS, row, col) for row, col in where]
-
-    for block, cross, source in ((DIFF, CPOS, pos), (VELO, CVEL, vel)):
-        for c in range(3):
-            values = at_ends(
-                lambda r: jnp.broadcast_to(source[c : c + 1, r * LANES : (r + 1) * LANES], (8, LANES))
-            )
-            for k in range(3):
-                put(block + END_ROWS * c, k, values[k] - values[3 + k])
-            pay[cross + CROSS_ROWS * c : cross + CROSS_ROWS * (c + 1), :] = values[6][:CROSS_ROWS]
-    values = at_ends(functools.partial(spread, mass))
+    def wide(source, c, r):
+        return jnp.broadcast_to(source[c : c + 1, r * LANES : (r + 1) * LANES], (8, LANES))
+
+    tables = [functools.partial(wide, source, c) for source in (pos, vel) for c in range(3)]
+    tables.append(functools.partial(spread, mass))
+
+    def at(k):
+        row, col = where[k]
+        return [gather_rows(table, ATOM_ROWS, row, col) for table in tables]
+
     for k in range(3):
-        put(MASS, k, values[k])
-        put(SCAL, k, 1.0 / jnp.sqrt(values[k] + values[3 + k]))
-    pay[CMAS : CMAS + CROSS_ROWS, :] = values[6][:CROSS_ROWS]
+        near, away = at(k), at(3 + k)
+        for c in range(6):
+            put(END_ROWS * c, k, near[c] - away[c])
+        put(MASS, k, near[6])
+        put(SCAL, k, 1.0 / jnp.sqrt(near[6] + away[6]))
+    for c, value in enumerate(at(6)):
+        pay[CPOS + CROSS_ROWS * c : CPOS + CROSS_ROWS * (c + 1), :] = value[:CROSS_ROWS]
 
 
 def solve(
@@ -763,6 +768,7 @@
             *(pltpu.VMEM(x.shape, x.dtype) for x in inputs),
             pltpu.VMEM((40, LANES), i32),
             pltpu.VMEM((32, LANES), f32),
+            pltpu.VMEM((24, LANES), f32),
             pltpu.VMEM((8, LANES), f32),
             pltpu.SemaphoreType.DMA((len(inputs),)),
         ],

time: 40.2 us -> 39.9 us (level)
  no operation moved by 1% of the time
where the time goes in v5:
time: 39.9 us; the launch traced here: 39.7 us
  Pallas kernels  19.8 us (50%)
  blocking collectives  19.1 us (48%)
  between operations  0.83 us (2%)
    all_gather x1, blocking collectives, on_device(): whole = lax.all_gather(pay, 'dom', axis=0, tiled=True)  19.1 us
    pallas_call x1, Pallas kernels, on_device(): pl.pallas_call(solve, out_specs=(pl.BlockSpec(memory_space=pltpu.VMEM), p...  16.1 us
    pallas_call x1, Pallas kernels, on_device(): pl.pallas_call(prepare, in_specs=[pl.BlockSpec(memory_space=pltpu.HBM)] *...  3.66 us

profile of v5, /device:TPU:1, one launch (start us, length us, event | category | flops | bytes accessed | tf_op | source)
XLA Modules:
  0.0 39.7 jit_solution(17621687881618765581)
XLA Ops:
  0.6 3.7 %prepare.1 = (f32[248,128]{1,0:T(8,128)S(1)}, s32[16,128]{1,0:T(8,128)S(1)}) custom-call(s32[2,1280]{1,0:T(2,128)} %bonds_in.1, s32[3,128]{1,0:T(4,128)} %bitcast.4, s32[3,128]{1,0:T(4,128)} %bitcast.5, f32[3,2048]{1,0:T(4,128)} %pos_in.1, f32[3,2048]{1,0:T(4,128)} %vel.1, f32[16,128]{1,0:T(8,128)} %bitcast.3), custom_call_target="tpu_custom_call" | custom-call | tf_op jit(solution)/shard_map/prepare/pallas_call | solution.py:760
  4.3 0.0 copy-start
  4.3 0.0 copy-start.1
  4.3 0.0 copy-start.2
  4.3 19.1 %all_gather.3.whole = f32[1984,128]{1,0:T(8,128)S(1)} all-gather(f32[248,128]{1,0:T(8,128)S(1)} %get-tuple-element.4), channel_id=1, replica_groups=mesh['rep'=32,'dom'=8] {'dom'}, dimensions={0}, use_global_device_ids=true | all-gather | bytes 1142784 | tf_op jit(solution)/shard_map/all_gather | solution.py:778
  23.5 0.0 copy-done
  23.5 0.0 copy-done.1
  23.5 0.0 copy-done.2
  23.5 16.1 %solve.1 = (f32[3,2048]{1,0:T(4,128)}, f32[9,1024]{1,0:T(8,128)}) custom-call(f32[1984,128]{1,0:T(8,128)S(1)} %all_gather.3.whole, s32[16,128]{1,0:T(8,128)S(1)} %get-tuple-element.5.place, f32[3,2048]{1,0:T(4,128)S(1)} %copy-done, f32[9,1024]{1,0:T(8,128)S(1)} %copy-done.1, f32[9,1024]{1,0:T(8,128)S(1)} %copy-done.2), custom_call_target="tpu_custom_call" | custom-call | tf_op jit(solution)/shard_map/solve/pallas_call | solution.py:784
Async XLA Ops:
  4.3 19.2 %copy-start = (f32[3,2048]{1,0:T(4,128)S(1)}, f32[3,2048]{1,0:T(4,128)}, u32[]{:S(2)}) copy-start(f32[3,2048]{1,0:T(4,128)} %vel.1) | copy-start | bytes 73732
  4.3 19.1 %copy-start.1 = (f32[9,1024]{1,0:T(8,128)S(1)}, f32[9,1024]{1,0:T(8,128)}, u32[]{:S(2)}) copy-start(f32[9,1024]{1,0:T(8,128)} %water_pos.1) | copy-start | bytes 110596
  4.3 19.1 %copy-start.2 = (f32[9,1024]{1,0:T(8,128)S(1)}, f32[9,1024]{1,0:T(8,128)}, u32[]{:S(2)}) copy-start(f32[9,1024]{1,0:T(8,128)} %water_vel.1) | copy-start | bytes 110596

commit v6 on v5

--- a/solution.py
+++ b/solution.py
@@ -705,8 +705,7 @@
             take(index, place_in, lambda v: source.at[v])
 
         def turn(turns, carry):
-            for order in range(ORDER):
-                apply(False)
+            lax.fori_loop(0, ORDER // 2, lambda order, carry: (apply(False), apply(False), carry)[2], 0)
             move(False)
             correct()
             return carry

time: 39.9 us -> 39.8 us (level)
  no operation moved by 1% of the time
where the time goes in v6:
time: 39.8 us; the launch traced here: 39.6 us
  Pallas kernels  19.8 us (50%)
  blocking collectives  19.1 us (48%)
  between operations  0.67 us (2%)
    all_gather x1, blocking collectives, on_device(): whole = lax.all_gather(pay, 'dom', axis=0, tiled=True)  19.1 us
    pallas_call x1, Pallas kernels, on_device(): pl.pallas_call(solve, out_specs=(pl.BlockSpec(memory_space=pltpu.VMEM), p...  16.2 us
    pallas_call x1, Pallas kernels, on_device(): pl.pallas_call(prepare, in_specs=[pl.BlockSpec(memory_space=pltpu.HBM)] *...  3.66 us

profile of v6, /device:TPU:1, one launch (start us, length us, event | category | flops | bytes accessed | tf_op | source)
XLA Modules:
  0.0 39.6 jit_solution(10452765581250395580)
XLA Ops:
  0.6 3.7 %prepare.1 = (f32[248,128]{1,0:T(8,128)S(1)}, s32[16,128]{1,0:T(8,128)S(1)}) custom-call(s32[2,1280]{1,0:T(2,128)} %bonds_in.1, s32[3,128]{1,0:T(4,128)} %bitcast.4, s32[3,128]{1,0:T(4,128)} %bitcast.5, f32[3,2048]{1,0:T(4,128)} %pos_in.1, f32[3,2048]{1,0:T(4,128)} %vel.1, f32[16,128]{1,0:T(8,128)} %bitcast.3), custom_call_target="tpu_custom_call" | custom-call | tf_op jit(solution)/shard_map/prepare/pallas_call | solution.py:759
  4.3 0.0 copy-start
  4.3 0.0 copy-start.1
  4.3 0.0 copy-start.2
  4.3 19.1 %all_gather.3.whole = f32[1984,128]{1,0:T(8,128)S(1)} all-gather(f32[248,128]{1,0:T(8,128)S(1)} %get-tuple-element.4), channel_id=1, replica_groups=mesh['rep'=32,'dom'=8] {'dom'}, dimensions={0}, use_global_device_ids=true | all-gather | bytes 1142784 | tf_op jit(solution)/shard_map/all_gather | solution.py:777
  23.5 0.0 copy-done
  23.5 0.0 copy-done.1
  23.5 0.0 copy-done.2
  23.5 16.2 %solve.1 = (f32[3,2048]{1,0:T(4,128)}, f32[9,1024]{1,0:T(8,128)}) custom-call(f32[1984,128]{1,0:T(8,128)S(1)} %all_gather.3.whole, s32[16,128]{1,0:T(8,128)S(1)} %get-tuple-element.5.place, f32[3,2048]{1,0:T(4,128)S(1)} %copy-done, f32[9,1024]{1,0:T(8,128)S(1)} %copy-done.1, f32[9,1024]{1,0:T(8,128)S(1)} %copy-done.2), custom_call_target="tpu_custom_call" | custom-call | tf_op jit(solution)/shard_map/solve/pallas_call | solution.py:783
Async XLA Ops:
  4.3 19.2 %copy-start = (f32[3,2048]{1,0:T(4,128)S(1)}, f32[3,2048]{1,0:T(4,128)}, u32[]{:S(2)}) copy-start(f32[3,2048]{1,0:T(4,128)} %vel.1) | copy-start | bytes 73732
  4.3 19.1 %copy-start.1 = (f32[9,1024]{1,0:T(8,128)S(1)}, f32[9,1024]{1,0:T(8,128)}, u32[]{:S(2)}) copy-start(f32[9,1024]{1,0:T(8,128)} %water_pos.1) | copy-start | bytes 110596
  4.3 19.1 %copy-start.2 = (f32[9,1024]{1,0:T(8,128)S(1)}, f32[9,1024]{1,0:T(8,128)}, u32[]{:S(2)}) copy-start(f32[9,1024]{1,0:T(8,128)} %water_vel.1) | copy-start | bytes 110596
